TPU v7x, 256 devices: a whole 4x4x8 slice. The times are simulated.
256 devices in a mesh: veh: 64 (over z, y, core), row: 4 (over x).
Axes of the slice: x: 4, y: 4, z: 8, core: 2. Of those that a mesh axis runs over, the one named last changes fastest.
Arguments:
- bev_maps: bfloat16 [512, 32, 64, 128], P('veh', 'row'), may hold values from -6 to 6
- senders: int32 [512, 4], replicated, may hold values from 0 to 511, as said below
- shifts: int32 [512, 4], replicated, may hold values from -1 to 1
- counts: int32 [512], replicated, may hold values from 1 to 4, as said below
- agent_query: bfloat16 [128, 128], replicated, may hold values from -0.5 to 0.5
- agent_keyvalue: bfloat16 [128, 256], replicated, may hold values from -0.5 to 0.5
- agent_out: bfloat16 [128, 128], replicated, may hold values from -0.5 to 0.5
- agent_scale: float32 [4], replicated, may hold values from 1 to 600
- conv_weight: float32 [3, 3, 256], replicated, may hold values from -1.5 to 1.5
- gain_first: float32 [256], replicated, may hold values from 0.1 to 1.9
- window_in: bfloat16 [256, 768], replicated, may hold values from -0.375 to 0.375
- window_out: bfloat16 [256, 256], replicated, may hold values from -0.375 to 0.375
- window_scale: float32 [8], replicated, may hold values from 1 to 600
- gain_second: float32 [256], replicated, may hold values from 0.1 to 1.9
- hidden_up: bfloat16 [256, 512], replicated, may hold values from -0.375 to 0.375
- hidden_down: bfloat16 [512, 256], replicated, may hold values from -0.25 to 0.25
Outputs:
- joined_map: bfloat16 [512, 32, 64, 256], P('veh', 'row')
Inputs may be any that keep to these rules, and one draw needn't show every extreme that they name: `senders`: never the receiver itself. Blocks are aligned runs of 8 vehicles; over the live pairs whose receiver lies in one block and whose sender lies in one block, the intersecting tiles (2 - |shift| a pair) number at most 2. Slots a < counts[r] of receiver r are live.
All inputs are finite; a program needn't handle non-finite values.
Results may differ from a plain program's by a relative error of at most 0.0095.
The roundings to bfloat16 on the way count: a program that leaves them out, or rounds other values in their place, can miss the bound.
Values may be sent and summed in bfloat16 or wider, within the bound.
A program may use at most 128 MiB of HBM per device.

v0:
```python
import jax
import jax.numpy as jnp
from jax import lax
from jax.sharding import PartitionSpec as P

TILE = 32
WIN = 8


exact_dot = lax.Precision.HIGHEST
norm_eps = 1e-05
unit_eps = 1e-06


def padded_2(cells, sides, width):
    for axis, dim in sides:
        count = lax.axis_size(axis)
        ends = count - 1
        head = lax.slice_in_dim(cells, 0, width, axis=dim)
        tail = lax.slice_in_dim(cells, cells.shape[dim] - width, cells.shape[dim], axis=dim)
        cells = jnp.concatenate(
            [
                lax.ppermute(tail, axis, [(i, (i + 1) % count) for i in range(ends)]),
                cells,
                lax.ppermute(head, axis, [((i + 1) % count, i) for i in range(ends)]),
            ],
            axis=dim,
        )
    return cells


def head_spread(tensor, head_count):
    feature_width = tensor.shape[-1]
    member = (
        jnp.arange(feature_width)[:, None] // (feature_width // head_count)
        == jnp.arange(head_count)[None, :]
    ).astype(jnp.float32)
    summed = jnp.dot(tensor, member, precision=exact_dot)
    return jnp.dot(summed, member.T, precision=exact_dot)


def unit_heads(tensor, head_count):
    return tensor / jnp.sqrt(head_spread(tensor * tensor, head_count) + unit_eps)


def join_agents(ego_map, own_keyvalue, sent_keyvalue, covered, agent_query, agent_out, agent_scale):
    channels = ego_map.shape[-1]
    head_count = agent_scale.shape[0]
    queries = unit_heads(
        jnp.dot(ego_map, agent_query, preferred_element_type=jnp.float32), head_count
    )
    all_kv = jnp.concatenate([own_keyvalue[:, None], sent_keyvalue], axis=1).astype(jnp.float32)
    key_part = unit_heads(all_kv[..., :channels], head_count)
    values = all_kv[..., channels:]
    scale_row = jnp.repeat(agent_scale, channels // head_count)
    scores = head_spread(queries[:, None] * key_part, head_count) * scale_row
    present = jnp.concatenate([jnp.ones_like(covered[:, :1]), covered], axis=1)[..., None]
    scores = jnp.where(present, scores, -1e30)
    row_top = jnp.max(scores, axis=1, keepdims=True)
    weight = jnp.where(present, jnp.exp(scores - row_top), 0.0)
    weight = weight / jnp.sum(weight, axis=1, keepdims=True)
    agent_mix = jnp.sum(weight * values, axis=1).astype(jnp.bfloat16)
    joined = jnp.dot(agent_mix, agent_out, preferred_element_type=jnp.float32).astype(jnp.bfloat16)
    return jnp.concatenate([ego_map, joined], axis=-1)


def layer_norm(tensor, gain):
    average = jnp.mean(tensor, axis=-1, keepdims=True)
    centred = tensor - average
    spread = jnp.mean(centred * centred, axis=-1, keepdims=True)
    return centred * lax.rsqrt(spread + norm_eps) * gain


def to_windows(tensor, head_count):
    batch_size, height, width_cells, feature_width = tensor.shape
    tensor = tensor.reshape(
        batch_size,
        height // WIN,
        WIN,
        width_cells // WIN,
        WIN,
        head_count,
        feature_width // head_count,
    )
    tensor = tensor.transpose(0, 1, 3, 5, 2, 4, 6)
    return tensor.reshape(
        batch_size,
        height // WIN,
        width_cells // WIN,
        head_count,
        WIN * WIN,
        feature_width // head_count,
    )


def from_windows(tensor, height, width_cells):
    batch_size = tensor.shape[0]
    head_count = tensor.shape[3]
    head_width = tensor.shape[-1]
    tensor = tensor.reshape(
        batch_size, height // WIN, width_cells // WIN, head_count, WIN, WIN, head_width
    )
    tensor = tensor.transpose(0, 1, 4, 2, 5, 3, 6)
    return tensor.reshape(batch_size, height, width_cells, head_count * head_width)


def window_layer(
    padded,
    conv_weight,
    gain_first,
    window_in,
    window_out,
    window_scale,
    gain_second,
    hidden_up,
    hidden_down,
):
    batch_size, height, width_cells, feature_width = padded.shape
    height = height - 2
    widened = jnp.pad(padded, ((0, 0), (0, 0), (1, 1), (0, 0))).astype(jnp.float32)
    mixed_sum = widened[:, 1 : height + 1, 1 : width_cells + 1]
    for row_step in range(3):
        for col_step in range(3):
            mixed_sum = (
                mixed_sum
                + widened[:, row_step : row_step + height, col_step : col_step + width_cells]
                * conv_weight[row_step, col_step]
            )
    hidden = layer_norm(mixed_sum, gain_first).astype(jnp.bfloat16)
    projected = jnp.dot(hidden, window_in, preferred_element_type=jnp.float32)
    head_count = window_scale.shape[0]
    queries = to_windows(unit_heads(projected[..., :feature_width], head_count), head_count)
    key_part = to_windows(
        unit_heads(projected[..., feature_width : 2 * feature_width], head_count), head_count
    )
    values = to_windows(projected[..., 2 * feature_width :].astype(jnp.bfloat16), head_count)
    scores = (
        jnp.einsum("bxyhqd,bxyhkd->bxyhqk", queries, key_part, precision=exact_dot)
        * window_scale[:, None, None]
    )
    row_top = jnp.max(scores, axis=-1, keepdims=True)
    weight = jnp.exp(scores - row_top)
    weight = (weight / jnp.sum(weight, axis=-1, keepdims=True)).astype(jnp.bfloat16)
    attended = jnp.einsum(
        "bxyhqk,bxyhkd->bxyhqd", weight, values, preferred_element_type=jnp.float32
    )
    attended = from_windows(attended, height, width_cells).astype(jnp.bfloat16)
    mixed_sum = mixed_sum + jnp.dot(attended, window_out, preferred_element_type=jnp.float32)
    hidden = layer_norm(mixed_sum, gain_second).astype(jnp.bfloat16)
    inner_act = jax.nn.silu(jnp.dot(hidden, hidden_up, preferred_element_type=jnp.float32)).astype(
        jnp.bfloat16
    )
    return (mixed_sum + jnp.dot(inner_act, hidden_down, preferred_element_type=jnp.float32)).astype(
        jnp.bfloat16
    )


def on_device(
    bev_maps,
    senders,
    shifts,
    counts,
    agent_query,
    agent_keyvalue,
    agent_out,
    agent_scale,
    conv_weight,
    gain_first,
    window_in,
    window_out,
    window_scale,
    gain_second,
    hidden_up,
    hidden_down,
):
    vehicles_here, height, width_cells, channels = bev_maps.shape
    agents = senders.shape[1]
    devices = lax.axis_size("veh")
    myself = lax.axis_index("veh")
    tile_cols = width_cells // TILE
    pair_count = vehicles_here * agents
    per_link = max(1, pair_count // devices)
    capacity = tile_cols * per_link
    cell_count = height * width_cells
    send_all = senders.reshape(devices, pair_count)
    shift_all = shifts.reshape(devices, pair_count)
    live_all = (jnp.arange(agents)[None, :] < counts[:, None]).reshape(devices, pair_count)
    tiles_all = jnp.where(live_all, tile_cols - jnp.abs(shift_all), 0)
    source_all = send_all // vehicles_here
    tile_step = jnp.arange(tile_cols, dtype=jnp.int32)
    outgoing = jnp.where(source_all == myself, tiles_all, 0)
    slot_start = jnp.cumsum(outgoing, axis=1) - outgoing
    occupied = tile_step[None, None, :] < outgoing[:, :, None]
    target = jnp.where(
        occupied,
        jnp.arange(devices, dtype=jnp.int32)[:, None, None] * capacity
        + slot_start[:, :, None]
        + tile_step,
        devices * capacity,
    )
    anchor = (
        (send_all % vehicles_here)[:, :, None] * tile_cols
        + jnp.maximum(shift_all, 0)[:, :, None]
        + tile_step
    )
    slot_table = (
        jnp.full((devices * capacity,), -1, jnp.int32)
        .at[target.reshape(-1)]
        .set(anchor.reshape(-1), mode="drop")
    )
    filled = slot_table >= 0
    chosen = jnp.maximum(slot_table, 0)
    row_index = jnp.arange(height)[None, :]
    own_keyvalue = jnp.dot(bev_maps, agent_keyvalue, preferred_element_type=jnp.float32).astype(
        jnp.bfloat16
    )
    feature_width = bev_maps.shape[-1]
    tiled_map = bev_maps.reshape(vehicles_here, height, tile_cols, TILE, feature_width)
    packed = tiled_map[(chosen // tile_cols)[:, None], row_index, (chosen % tile_cols)[:, None]]
    packed = jnp.where(filled[:, None, None, None], packed, jnp.zeros((), bev_maps.dtype))
    arrived = jnp.dot(
        lax.all_to_all(
            packed.reshape(devices, capacity, height, TILE, feature_width),
            "veh",
            split_axis=0,
            concat_axis=0,
            tiled=True,
        ),
        agent_keyvalue,
        preferred_element_type=jnp.float32,
    ).astype(jnp.bfloat16)
    arrived = arrived.reshape(devices * capacity, height, TILE, 2 * channels)
    my_senders = send_all[myself]
    my_shifts = shift_all[myself]
    my_tiles = tiles_all[myself]
    my_live = live_all[myself]
    my_sources = my_senders // vehicles_here
    position = jnp.arange(pair_count)
    earlier = (my_sources[None, :] == my_sources[:, None]) & (position[None, :] < position[:, None])
    offset = jnp.sum(jnp.where(earlier, my_tiles[None, :], 0), axis=1)
    shifted = tile_step[None, :] + my_shifts[:, None]
    inside = (shifted >= 0) & (shifted < tile_cols) & my_live[:, None]
    slot_of = (
        my_sources[:, None] * capacity
        + offset[:, None]
        + tile_step[None, :]
        - jnp.maximum(-my_shifts, 0)[:, None]
    )
    slot_of = jnp.where(inside, slot_of, 0)
    covered_cols = jnp.repeat(inside, TILE, axis=1)
    group_size = min(vehicles_here, max(1, 1024 // cell_count))
    block_count = vehicles_here // group_size
    band_rows = jnp.arange(height)[None, :, None]

    def agent_group(operands):
        ego_map, self_kv, group_slots, group_cover = operands
        sent_keyvalue = arrived[group_slots[:, None, :], band_rows]
        sent_keyvalue = sent_keyvalue.reshape(group_size, agents, cell_count, 2 * channels)
        covered = jnp.broadcast_to(
            group_cover.reshape(group_size, agents, 1, width_cells),
            (group_size, agents, height, width_cells),
        ).reshape(group_size, agents, cell_count)
        mixed_in = join_agents(
            ego_map.reshape(group_size, cell_count, channels),
            self_kv.reshape(group_size, cell_count, 2 * channels),
            sent_keyvalue,
            covered,
            agent_query,
            agent_out,
            agent_scale,
        )
        return mixed_in.reshape(group_size, height, width_cells, 2 * channels)

    layer_input = lax.map(
        agent_group,
        (
            bev_maps.reshape(block_count, group_size, height, width_cells, channels),
            own_keyvalue.reshape(block_count, group_size, height, width_cells, 2 * channels),
            slot_of.reshape(block_count, group_size * agents, tile_cols),
            covered_cols.reshape(block_count, group_size * agents, width_cells),
        ),
    )
    layer_input = layer_input.reshape(vehicles_here, height, width_cells, 2 * channels)
    padded = padded_2(layer_input, (("row", 1),), 1)

    def layer_group(padded_group):
        return window_layer(
            padded_group,
            conv_weight,
            gain_first,
            window_in,
            window_out,
            window_scale,
            gain_second,
            hidden_up,
            hidden_down,
        )

    result = lax.map(
        layer_group, padded.reshape(block_count, group_size, height + 2, width_cells, 2 * channels)
    )
    return result.reshape(vehicles_here, height, width_cells, 2 * channels)


def solution(mesh):
    in_specs = (
        P("veh", "row", None, None),
        P(),
        P(),
        P(),
        P(),
        P(),
        P(),
        P(),
        P(),
        P(),
        P(),
        P(),
        P(),
        P(),
        P(),
        P(),
    )
    out_specs = P("veh", "row", None, None)
    return jax.shard_map(
        on_device, mesh=mesh, in_specs=in_specs, out_specs=out_specs, check_vma=False
    )
```

profile of v0, /device:TPU:1, one launch (start us, length us, event | category | flops | bytes accessed | tf_op | source)
XLA Modules:
  0.0 569.5 jit_solution(4987634288585464732)
XLA Ops:
  5.5 15.5 %scatter_custom_fusion = s32[128]{0:T(128)S(1)} fusion(s32[4096]{0:T(1024)S(1)} %bitcast.278, s32[4096]{0:T(1024)S(1)} %reshape.683, s32[]{:T(128)} %constant.272.clone.1), kind=kCustom, calls=%fused_computation.206 | custom fusion | bytes 516 | tf_op jit(solution)/shard_map/scatter | solution.py:209
  21.4 12.7 %gather_fusion.1 = bf16[1024,32,128]{2,1,0:T(8,128)(2,1)} fusion(bf16[8,8,2,32,128]{4,3,2,1,0:T(8,128)(2,1)S(1)} %bitcast.256, s32[1024]{0:T(1024)S(1)} %reshape.673), kind=kCustom, calls=%fused_computation.1 | custom fusion | bytes 16789504 | tf_op jit(solution)/shard_map/gather | solution.py:219
  34.1 7.2 %broadcast_select_fusion = bf16[64,2,8,32,128]{4,3,2,1,0:T(8,128)(2,1)} fusion(bf16[64,2,8,32,128]{4,3,2,1,0:T(8,128)(2,1)} %bitcast.261, pred[64,2]{1,0:T(8,128)(4,1)S(1)} %broadcast_in_dim.191), kind=kLoop, calls=%fused_computation.141 | loop fusion | flops 4194304 | bytes 16777344 | tf_op jit(solution)/shard_map/jit(_where)/select_n | solution.py:220
  41.3 13.3 %all-to-all-start = ((bf16[64,2,8,32,128]{4,3,2,1,0:T(8,128)(2,1)}), bf16[64,2,8,32,128]{4,3,2,1,0:T(8,128)(2,1)}, u32[]{:S(2)}, u32[]{:S(2)}) async-start(bf16[64,2,8,32,128]{4,3,2,1,0:T(8,128)(2,1)} %broadcast_select_fusion), calls=%async_computation | async-start | bytes 16777216 | tf_op jit(solution)/shard_map/all_to_all | solution.py:222
  57.7 179.2 %all-to-all-done = bf16[64,2,8,32,128]{4,3,2,1,0:T(8,128)(2,1)} async-done(((bf16[64,2,8,32,128]{4,3,2,1,0:T(8,128)(2,1)}), bf16[64,2,8,32,128]{4,3,2,1,0:T(8,128)(2,1)}, u32[]{:S(2)}, u32[]{:S(2)}) %all-to-all-start) | async-done | bytes 8388640 | tf_op jit(solution)/shard_map/all_to_all | solution.py:222
  237.0 13.6 %convolution_convert_fusion.1 = bf16[64,2,8,32,256]{4,3,2,1,0:T(8,128)(2,1)} fusion(bf16[64,2,8,32,128]{4,3,2,1,0:T(8,128)(2,1)} %all-to-all-done, bf16[128,256]{1,0:T(8,128)(2,1)S(1)} %copy-done), kind=kOutput, calls=%fused_computation.140 | convolution fusion | flops 2155872256 | bytes 25231360 | tf_op jit(solution)/shard_map/dot_general | solution.py:221
  252.1 89.8 %while.26 = (s32[]{:T(128)}, bf16[4,2,8,64,256]{4,3,2,1,0:T(8,128)(2,1)}, bf16[4,2,8,64,128]{4,3,2,1,0:T(8,128)(2,1)S(1)}, pred[4,8,64]{2,1,0:T(8,128)(4,1)S(1)}...) while((s32[]{:T(128)}, ...), condition=%wide.region_7.8_spmd.clone, body=%wide.region_3.7_spmd.clone.sunk | while | flops 221778144 | bytes 86457960 | solution.py:274
  254.8 6.6 %gather_fusion = bf16[128,32,256]{2,1,0:T(8,128)(2,1)S(1)} fusion(bf16[128,8,32,256]{3,2,1,0:T(8,128)(2,1)} %get-tuple-element.574, s32[128]{0:T(128)S(1)} %reshape.741), kind=kCustom, calls=%fused_computation.clone.clone.1 | custom fusion | bytes 4195328 | tf_op jit(solution)/shard_map/while/body/eval_jaxpr/gather | solution.py:257
  277.1 6.6 %gather_fusion = bf16[128,32,256]{2,1,0:T(8,128)(2,1)S(1)} fusion(bf16[128,8,32,256]{3,2,1,0:T(8,128)(2,1)} %get-tuple-element.574, s32[128]{0:T(128)S(1)} %reshape.741), kind=kCustom, calls=%fused_computation.clone.clone.1 | custom fusion | bytes 4195328 | tf_op jit(solution)/shard_map/while/body/eval_jaxpr/gather | solution.py:257
  299.5 6.6 %gather_fusion = bf16[128,32,256]{2,1,0:T(8,128)(2,1)S(1)} fusion(bf16[128,8,32,256]{3,2,1,0:T(8,128)(2,1)} %get-tuple-element.574, s32[128]{0:T(128)S(1)} %reshape.741), kind=kCustom, calls=%fused_computation.clone.clone.1 | custom fusion | bytes 4195328 | tf_op jit(solution)/shard_map/while/body/eval_jaxpr/gather | solution.py:257
  321.9 6.6 %gather_fusion = bf16[128,32,256]{2,1,0:T(8,128)(2,1)S(1)} fusion(bf16[128,8,32,256]{3,2,1,0:T(8,128)(2,1)} %get-tuple-element.574, s32[128]{0:T(128)S(1)} %reshape.741), kind=kCustom, calls=%fused_computation.clone.clone.1 | custom fusion | bytes 4195328 | tf_op jit(solution)/shard_map/while/body/eval_jaxpr/gather | solution.py:257
  349.5 3.8 collective-permute-done.1
  358.5 210.0 %while.25 = (s32[]{:T(128)}, bf16[4,2,8,64,256]{4,3,2,1,0:T(8,128)(2,1)}, bf16[4,2,10,64,256]{4,3,2,1,0:T(8,128)(2,1)}, f32[3,3,256]{2,1,0:T(4,128)S(1)}, f32[25...) while((s32[]{:T(128)}, ...), condition=%wide.region_15.16_spmd, body=%wide.region_8.15_spmd.sunk | while | flops 1426937856 | bytes 66022180 | solution.py:299
  387.0 11.4 %fusion.222 = f32[2,8,8,64,64]{3,4,2,1,0:T(8,128)S(1)} fusion(f32[2,1,8,8,8,8,32]{6,5,4,3,2,0,1:T(8,128)} %reshape.737, f32[2,1,8,8,8,8,32]{6,5,4,3,2,0,1:T(8,128)} %reshape.738), kind=kOutput, calls=%fused_computation.5.clone.1 | convolution fusion | flops 201326592 | bytes 4194304 | tf_op jit(solution)/shard_map/while/body/eval_jaxpr/bxyhqd,bxyhkd->bxyhqk/dot_general | solution.py:138
  405.1 3.9 fusion.224
  411.0 3.8 copy.118
  436.3 11.4 %fusion.222 = f32[2,8,8,64,64]{3,4,2,1,0:T(8,128)S(1)} fusion(f32[2,1,8,8,8,8,32]{6,5,4,3,2,0,1:T(8,128)} %reshape.737, f32[2,1,8,8,8,8,32]{6,5,4,3,2,0,1:T(8,128)} %reshape.738), kind=kOutput, calls=%fused_computation.5.clone.1 | convolution fusion | flops 201326592 | bytes 4194304 | tf_op jit(solution)/shard_map/while/body/eval_jaxpr/bxyhqd,bxyhkd->bxyhqk/dot_general | solution.py:138
  454.4 3.9 fusion.224
  460.3 3.8 copy.118
  485.7 11.4 %fusion.222 = f32[2,8,8,64,64]{3,4,2,1,0:T(8,128)S(1)} fusion(f32[2,1,8,8,8,8,32]{6,5,4,3,2,0,1:T(8,128)} %reshape.737, f32[2,1,8,8,8,8,32]{6,5,4,3,2,0,1:T(8,128)} %reshape.738), kind=kOutput, calls=%fused_computation.5.clone.1 | convolution fusion | flops 201326592 | bytes 4194304 | tf_op jit(solution)/shard_map/while/body/eval_jaxpr/bxyhqd,bxyhkd->bxyhqk/dot_general | solution.py:138
  503.7 3.9 fusion.224
  509.7 3.8 copy.118
  535.0 11.4 %fusion.222 = f32[2,8,8,64,64]{3,4,2,1,0:T(8,128)S(1)} fusion(f32[2,1,8,8,8,8,32]{6,5,4,3,2,0,1:T(8,128)} %reshape.737, f32[2,1,8,8,8,8,32]{6,5,4,3,2,0,1:T(8,128)} %reshape.738), kind=kOutput, calls=%fused_computation.5.clone.1 | convolution fusion | flops 201326592 | bytes 4194304 | tf_op jit(solution)/shard_map/while/body/eval_jaxpr/bxyhqd,bxyhkd->bxyhqk/dot_general | solution.py:138
  553.1 3.9 fusion.224
  (340 shorter events, 210.7 us)
Async XLA Ops:
  0.0 55.6 %copy-start = (bf16[128,256]{1,0:T(8,128)(2,1)S(1)}, bf16[128,256]{1,0:T(8,128)(2,1)}, u32[]{:S(2)}) copy-start(bf16[128,256]{1,0:T(8,128)(2,1)} %param.25) | copy-start | bytes 196612
  1.9 19.6 %copy-start.6 = (bf16[8,8,64,128]{3,2,1,0:T(8,128)(2,1)S(1)}, bf16[8,8,64,128]{3,2,1,0:T(8,128)(2,1)}, u32[]{:S(2)}) copy-start(bf16[8,8,64,128]{3,2,1,0:T(8,128)(2,1)} %param.20) | copy-start | bytes 3145732
  41.3 195.6 %all-to-all-start = ((bf16[64,2,8,32,128]{4,3,2,1,0:T(8,128)(2,1)}), bf16[64,2,8,32,128]{4,3,2,1,0:T(8,128)(2,1)}, u32[]{:S(2)}, u32[]{:S(2)}) async-start(bf16[64,2,8,32,128]{4,3,2,1,0:T(8,128)(2,1)} %broadcast_select_fusion), calls=%async_computation | async-start | bytes 16777216 | tf_op jit(solution)/shard_map/all_to_all | solution.py:222
  57.7 194.4 %copy-start.10 = (bf16[128,128]{1,0:T(8,128)(2,1)S(1)}, bf16[128,128]{1,0:T(8,128)(2,1)}, u32[]{:S(2)}) copy-start(bf16[128,128]{1,0:T(8,128)(2,1)} %param.24) | copy-start | bytes 98308
  57.7 194.4 %copy-start.11 = (bf16[128,128]{1,0:T(8,128)(2,1)S(1)}, bf16[128,128]{1,0:T(8,128)(2,1)}, u32[]{:S(2)}) copy-start(bf16[128,128]{1,0:T(8,128)(2,1)} %param.26) | copy-start | bytes 98308
  57.7 194.4 %copy-start.15 = (f32[4]{0:T(128)S(1)}, f32[4]{0:T(128)}, u32[]{:S(2)}) copy-start(f32[4]{0:T(128)} %param.27) | copy-start | bytes 52
  343.0 6.4 %collective-permute-start = (bf16[8,1,64,256]{3,2,1,0:T(8,128)(2,1)S(1)}, bf16[8,1,64,256]{3,2,1,0:T(8,128)(2,1)S(1)}, u32[]{:S(2)}, u32[]{:S(2)}) collective-permute-start(bf16[8,1,64,256]{3,2,1,0:T(8,128)(2,1)S(1)} %get-tuple-element.368), channel_id=1, source_target_pairs={{0,1},{1,2},{2,3},{4,5},{5,6},{6,7},{8,9},{9,10},{10,11},{12,13},{... | collective-permute-start | bytes 786440 | tf_op jit(solution)/shard_map/ppermute | solution.py:23
  346.2 7.1 %collective-permute-start.1 = (bf16[8,1,64,256]{3,2,1,0:T(8,128)(2,1)S(1)}, bf16[8,1,64,256]{3,2,1,0:T(8,128)(2,1)S(1)}, u32[]{:S(2)}, u32[]{:S(2)}) collective-permute-start(bf16[8,1,64,256]{3,2,1,0:T(8,128)(2,1)S(1)} %get-tuple-element.369), channel_id=1, source_target_pairs={{1,0},{2,1},{3,2},{5,4},{6,5},{7,6},{9,8},{10,9},{11,10},{13,12},{... | collective-permute-start | bytes 786440 | tf_op jit(solution)/shard_map/ppermute | solution.py:25
  353.3 5.2 copy-start.9
  353.3 5.2 copy-start.12
  353.3 5.2 copy-start.13
  353.3 5.2 copy-start.14
  353.3 5.2 copy-start.18
  411.0 7.0 %copy-start.5 = (f32[2,8,64,256]{3,2,1,0:T(8,128)S(1)}, f32[2,8,64,256]{3,2,1,0:T(8,128)}, u32[]{:S(2)}) copy-start(f32[2,8,64,256]{3,2,1,0:T(8,128)} %copy-done.4) | copy-start | bytes 3145732 | tf_op jit(solution)/shard_map/while
  414.8 4.0 copy-start.17
  460.3 7.0 %copy-start.5 = (f32[2,8,64,256]{3,2,1,0:T(8,128)S(1)}, f32[2,8,64,256]{3,2,1,0:T(8,128)}, u32[]{:S(2)}) copy-start(f32[2,8,64,256]{3,2,1,0:T(8,128)} %copy-done.4) | copy-start | bytes 3145732 | tf_op jit(solution)/shard_map/while
  464.1 4.0 copy-start.16
  464.1 4.0 copy-start.17
  509.6 7.0 %copy-start.5 = (f32[2,8,64,256]{3,2,1,0:T(8,128)S(1)}, f32[2,8,64,256]{3,2,1,0:T(8,128)}, u32[]{:S(2)}) copy-start(f32[2,8,64,256]{3,2,1,0:T(8,128)} %copy-done.4) | copy-start | bytes 3145732 | tf_op jit(solution)/shard_map/while
  513.4 4.0 copy-start.16
  513.4 4.0 copy-start.17
  559.0 7.0 %copy-start.5 = (f32[2,8,64,256]{3,2,1,0:T(8,128)S(1)}, f32[2,8,64,256]{3,2,1,0:T(8,128)}, u32[]{:S(2)}) copy-start(f32[2,8,64,256]{3,2,1,0:T(8,128)} %copy-done.4) | copy-start | bytes 3145732 | tf_op jit(solution)/shard_map/while
  562.8 4.0 copy-start.16
  562.8 4.0 copy-start.17
  (22 other events, 60.1 us)
where the time goes:
time: 579 us; the launch traced here: 570 us
  waiting for transfers between devices  185 us (32%)
  local copies, waits for them, and re-layouts  156 us (27%)
  matrix products  148 us (26%)
  other arithmetic  48 us (8%)
  starting transfers between devices  17.8 us (3%)
  loops' own time  14.1 us (2%)
    all_to_all x1, waiting for transfers between devices, on_device(): lax.all_to_all(packed.reshape(devices, capacity, height, TILE, feature_wi...  179 us
    dot_general x4, matrix products, window_layer(): jnp.einsum('bxyhqd,bxyhkd->bxyhqk', queries, key_part, precision=exact_dot)  45.5 us
    reshape x12, local copies, waits for them, and re-layouts, to_windows(): tensor.reshape(batch_size, height // WIN, WIN, width_cells // WIN, WIN, h...  40.4 us
    dot_general x20, matrix products, head_spread(): return jnp.dot(summed, member.T, precision=exact_dot)  38.9 us
    convert_element_type x12, local copies, waits for them, and re-layouts, window_layer(): attended = from_windows(attended, height, width_cells).astype(jnp.bfloat16)  35.8 us
    gather x4, local copies, waits for them, and re-layouts, agent_group(): sent_keyvalue = arrived[group_slots[:, None, :], band_rows]  26.5 us
    dot_general x20, matrix products, head_spread(): summed = jnp.dot(tensor, member, precision=exact_dot)  19.9 us
    dot_general x4, matrix products, window_layer(): jnp.einsum('bxyhqk,bxyhkd->bxyhqd', weight, values, preferred_element_typ...  15.6 us
  transfers between devices with their start and end apart: 3, of which 3 were waited for; matrix products, arithmetic and copies ran while one was open for 1% of the time, Pallas kernels for 0%

commit v1 on v0

v1 whole, which is shorter than its diff:
```python
import functools
import jax
import jax.numpy as jnp
from jax import lax
from jax.experimental import pallas as pl
from jax.experimental.pallas import tpu as pltpu
from jax.sharding import PartitionSpec as P

TILE = 32
WIN = 8
HEAD = 32
norm_eps = 1e-05
unit_eps = 1e-06
f32 = jnp.float32
bf16 = jnp.bfloat16


def nt_dot(a, b):
    return lax.dot_general(a, b, (((1,), (1,)), ((), ())), preferred_element_type=f32)


def halves(x):
    high = x.astype(bf16)
    return high, (x - high.astype(f32)).astype(bf16)


def head_sums(x, member):
    return jnp.dot(jnp.concatenate(halves(x), axis=-1), member, preferred_element_type=f32)


def agent_kernel(slot_ref, live_ref, ego_ref, t0, t1, t2, t3, query_ref, keyvalue_ref, out_w_ref,
                 scale_ref, member_ref, joined_ref):
    step = pl.program_id(0)
    tiles = (t0, t1, t2, t3)
    height, cols, channels = ego_ref.shape[1:]
    cells = height * cols
    ego = ego_ref[0].reshape(cells, channels)
    member = member_ref[...]
    query = jnp.dot(ego, query_ref[...], preferred_element_type=f32)
    query = query * (lax.rsqrt(head_sums(query * query, member) + unit_eps) * scale_ref[...])
    scores, values = [], []
    for a in range(len(tiles) + 1):
        source = ego if a == 0 else tiles[a - 1][0].reshape(cells, channels)
        keyvalue = jnp.dot(source, keyvalue_ref[...], preferred_element_type=f32).astype(bf16)
        key = keyvalue[:, :channels].astype(f32)
        values.append(keyvalue[:, channels:])
        score = head_sums(query * key, member) * lax.rsqrt(head_sums(key * key, member) + unit_eps)
        if a:
            score = score + jnp.where(live_ref[step * len(tiles) + a - 1] > 0, 0.0, -1e30)
        scores.append(score)
    top = functools.reduce(jnp.maximum, scores)
    total, mix = None, None
    for score, value in zip(scores, values):
        weight = jnp.exp(score - top)
        total = weight if total is None else total + weight
        part = weight * value.astype(f32)
        mix = part if mix is None else mix + part
    mix = (mix / total).astype(bf16)
    joined = jnp.dot(mix, out_w_ref[...], preferred_element_type=f32).astype(bf16)
    joined_ref[0] = joined.reshape(height, cols, channels)


def member_matrix(width):
    rows = jnp.arange(2 * width)[:, None] % width // HEAD
    return (rows == jnp.arange(width)[None, :] // HEAD).astype(bf16)


def agent_stage(bev_maps, arrived, slots, live, agent_query, agent_keyvalue, agent_out, agent_scale):
    vehicles, height, width_cells, channels = bev_maps.shape
    tile_cols = width_cells // TILE
    agents = slots.shape[1]
    full = lambda i, *_: (0, 0)
    ego_spec = pl.BlockSpec((1, height, TILE, channels), lambda i, *_: (i // tile_cols, 0, i % tile_cols, 0))
    tile_specs = [
        pl.BlockSpec((1, height, TILE, channels), lambda i, s, l, a=a: (s[i * agents + a], 0, 0, 0))
        for a in range(agents)
    ]
    scale_row = jnp.repeat(agent_scale, channels // agent_scale.shape[0])[None]
    return pl.pallas_call(
        agent_kernel,
        grid_spec=pltpu.PrefetchScalarGridSpec(
            num_scalar_prefetch=2,
            grid=(vehicles * tile_cols,),
            in_specs=[ego_spec, *tile_specs]
            + [pl.BlockSpec(w.shape, full) for w in (agent_query, agent_keyvalue, agent_out)]
            + [pl.BlockSpec((1, channels), full), pl.BlockSpec((2 * channels, channels), full)],
            out_specs=ego_spec,
        ),
        out_shape=jax.ShapeDtypeStruct(bev_maps.shape, bf16),
        compiler_params=pltpu.CompilerParams(dimension_semantics=("arbitrary",)),
        name="agent_stage",
    )(slots.reshape(-1), live.reshape(-1), bev_maps, arrived, arrived, arrived, arrived, agent_query,
      agent_keyvalue, agent_out, scale_row, member_matrix(channels))


def layer_norm(x, gain):
    centred = x - jnp.mean(x, axis=-1, keepdims=True)
    spread = jnp.mean(centred * centred, axis=-1, keepdims=True)
    return (centred * lax.rsqrt(spread + norm_eps) * gain).astype(bf16)


def layer_kernel(bev_ref, joined_ref, bev_up, bev_down, joined_up, joined_down, conv_ref, gain1_ref,
                 in_ref, out_w_ref, scale_ref, gain2_ref, up_ref, down_ref, member_ref, out_ref,
                 mixed_ref, attended_ref):
    height, cols, channels = bev_ref.shape[1:]
    cells = height * cols
    windows = cols // WIN
    area = WIN * WIN
    width = 2 * channels
    column = lax.broadcasted_iota(jnp.int32, (cells, channels), 0) % cols
    for half, (main, top, bottom) in enumerate(
        ((bev_ref, bev_up, bev_down), (joined_ref, joined_up, joined_down))
    ):
        lanes = slice(half * channels, (half + 1) * channels)
        rows = jnp.concatenate([top[0], main[0], bottom[0]], axis=0).astype(f32)
        sums = []
        for dj in range(3):
            taps = [conv_ref[di * 3 + dj : di * 3 + dj + 1, lanes] for di in range(3)]
            if dj == 1:
                taps[1] = taps[1] + 1.0
            acc = rows[0:height] * taps[0] + rows[1 : height + 1] * taps[1] + rows[2:] * taps[2]
            sums.append(acc.reshape(cells, channels))
        mixed = (
            sums[1]
            + jnp.where(column == 0, 0.0, pltpu.roll(sums[0], 1, axis=0))
            + jnp.where(column == cols - 1, 0.0, pltpu.roll(sums[2], cells - 1, axis=0))
        )
        for r in range(height):
            for w in range(windows):
                mixed_ref[w * area + r * WIN : w * area + (r + 1) * WIN, lanes] = mixed[
                    r * cols + w * WIN : r * cols + (w + 1) * WIN
                ]
    mixed = mixed_ref[...]
    hidden = layer_norm(mixed, gain1_ref[...])
    projected = jnp.dot(hidden, in_ref[...], preferred_element_type=f32)
    member = member_ref[...]
    groups = []
    for g in range(width // channels):
        lanes = slice(g * channels, (g + 1) * channels)
        query = projected[:, g * channels : (g + 1) * channels]
        key = projected[:, width + g * channels : width + (g + 1) * channels]
        query = query * (lax.rsqrt(head_sums(query * query, member) + unit_eps) * scale_ref[:, lanes])
        key = key * lax.rsqrt(head_sums(key * key, member) + unit_eps)
        value = projected[:, 2 * width + g * channels : 2 * width + (g + 1) * channels].astype(bf16)
        groups.append((jnp.concatenate(halves(query), axis=-1), *halves(key), value))
    heads = channels // HEAD
    head_of = lax.broadcasted_iota(jnp.int32, (area, 2 * channels), 1) % channels // HEAD
    lane_head = lax.broadcasted_iota(jnp.int32, (area, channels), 1) // HEAD
    for w in range(windows):
        span = slice(w * area, (w + 1) * area)
        for g, (query, key_high, key_low, value) in enumerate(groups):
            q = query[span]
            spread_q = jnp.concatenate(
                [jnp.where(head_of == j, q, jnp.zeros_like(q)) for j in range(heads)], axis=0
            )
            kh = key_high[span]
            scores = nt_dot(jnp.concatenate([kh, kh], axis=-1), spread_q) + nt_dot(
                key_low[span], spread_q[:, :channels]
            )
            weight = jnp.exp(scores - jnp.max(scores, axis=0, keepdims=True))
            weight = weight * (1.0 / jnp.sum(weight, axis=0, keepdims=True))
            mixed_values = jnp.dot(weight.T.astype(bf16), value[span], preferred_element_type=f32)
            attended = jnp.where(lane_head == 0, mixed_values[:area], 0.0)
            for j in range(1, heads):
                attended = jnp.where(lane_head == j, mixed_values[j * area : (j + 1) * area], attended)
            attended_ref[span, g * channels : (g + 1) * channels] = attended.astype(bf16)
    mixed = mixed + jnp.dot(attended_ref[...], out_w_ref[...], preferred_element_type=f32)
    hidden = layer_norm(mixed, gain2_ref[...])
    inner = jnp.dot(hidden, up_ref[...], preferred_element_type=f32)
    inner = (inner / (1.0 + jnp.exp(-inner))).astype(bf16)
    result = mixed + jnp.dot(inner, down_ref[...], preferred_element_type=f32)
    for r in range(height):
        for w in range(0, windows, 2):
            pair = [result[v * area + r * WIN : v * area + (r + 1) * WIN] for v in (w, w + 1)]
            out_ref[0, r, w * WIN : (w + 2) * WIN, :] = jnp.concatenate(pair, axis=0).astype(bf16)


def layer_stage(bev_maps, joined, bev_halo, joined_halo, conv_weight, gain_first, window_in, window_out,
                window_scale, gain_second, hidden_up, hidden_down):
    vehicles, height, width_cells, channels = bev_maps.shape
    width = 2 * channels
    cells = height * width_cells
    block = pl.BlockSpec((1, height, width_cells, channels), lambda i: (i, 0, 0, 0))
    edge = pl.BlockSpec((1, 1, width_cells, channels), lambda i: (i, 0, 0, 0))
    small = (
        conv_weight.reshape(9, width),
        gain_first[None],
        window_in,
        window_out,
        jnp.repeat(window_scale, width // window_scale.shape[0])[None],
        gain_second[None],
        hidden_up,
        hidden_down,
        member_matrix(channels),
    )
    return pl.pallas_call(
        layer_kernel,
        grid=(vehicles,),
        in_specs=[block, block, edge, edge, edge, edge]
        + [pl.BlockSpec(w.shape, lambda i: (0, 0)) for w in small],
        out_specs=pl.BlockSpec((1, height, width_cells, width), lambda i: (i, 0, 0, 0)),
        out_shape=jax.ShapeDtypeStruct((vehicles, height, width_cells, width), bf16),
        scratch_shapes=[pltpu.VMEM((cells, width), f32), pltpu.VMEM((cells, width), bf16)],
        compiler_params=pltpu.CompilerParams(dimension_semantics=("arbitrary",)),
        name="layer_stage",
    )(bev_maps, joined, *bev_halo, *joined_halo, *small)


def pack_kernel(pick_ref, maps_ref, packed_ref):
    count = packed_ref.shape[0]
    base = pl.program_id(0) * count
    for k in range(count):
        pick = pick_ref[base + k]
        col = pl.multiple_of((pick % 2) * TILE, TILE)
        packed_ref[k] = maps_ref[pick // 2, :, pl.ds(col, TILE), :]


def pack_tiles(bev_maps, picks, per_step=8):
    vehicles, height, width_cells, channels = bev_maps.shape
    slots = picks.shape[0]
    return pl.pallas_call(
        pack_kernel,
        grid_spec=pltpu.PrefetchScalarGridSpec(
            num_scalar_prefetch=1,
            grid=(slots // per_step,),
            in_specs=[pl.BlockSpec(bev_maps.shape, lambda i, *_: (0, 0, 0, 0))],
            out_specs=pl.BlockSpec((per_step, height, TILE, channels), lambda i, *_: (i, 0, 0, 0)),
        ),
        out_shape=jax.ShapeDtypeStruct((slots, height, TILE, channels), bf16),
        compiler_params=pltpu.CompilerParams(dimension_semantics=("arbitrary",)),
        name="pack_tiles",
    )(picks, bev_maps)


def row_halo(cells):
    count = lax.axis_size("row")
    height = cells.shape[1]
    return (
        lax.ppermute(cells[:, height - 1 :], "row", [(i, i + 1) for i in range(count - 1)]),
        lax.ppermute(cells[:, :1], "row", [(i + 1, i) for i in range(count - 1)]),
    )


def on_device(bev_maps, senders, shifts, counts, agent_query, agent_keyvalue, agent_out, agent_scale,
              conv_weight, gain_first, window_in, window_out, window_scale, gain_second, hidden_up,
              hidden_down):
    vehicles_here, height, width_cells, channels = bev_maps.shape
    agents = senders.shape[1]
    devices = lax.axis_size("veh")
    myself = lax.axis_index("veh")
    tile_cols = width_cells // TILE
    pair_count = vehicles_here * agents
    capacity = 2
    send_all = senders.reshape(devices, pair_count)
    shift_all = shifts.reshape(devices, pair_count)
    live_all = (jnp.arange(agents)[None, :] < counts[:, None]).reshape(devices, pair_count)
    tiles_all = jnp.where(live_all, tile_cols - jnp.abs(shift_all), 0)
    source_all = send_all // vehicles_here
    outgoing = jnp.where(source_all == myself, tiles_all, 0)
    before = (jnp.arange(pair_count)[:, None] < jnp.arange(pair_count)[None, :]).astype(f32)
    slot_start = jnp.dot(outgoing.astype(f32), before).astype(jnp.int32)
    base = (send_all % vehicles_here) * tile_cols + jnp.maximum(shift_all, 0)
    slot = jnp.arange(capacity)[None, :, None]
    step = slot - slot_start[:, None, :]
    hit = (step >= 0) & (step < outgoing[:, None, :])
    picks = jnp.sum(jnp.where(hit, base[:, None, :] + step, 0), axis=2).reshape(-1)
    packed = pack_tiles(bev_maps, picks).reshape(devices, capacity, height, TILE, channels)
    arrived = lax.all_to_all(packed, "veh", split_axis=0, concat_axis=0, tiled=True)
    arrived = arrived.reshape(devices * capacity, height, TILE, channels)

    tile_step = jnp.arange(tile_cols, dtype=jnp.int32)
    my_sources = source_all[myself]
    my_shifts = shift_all[myself]
    my_tiles = tiles_all[myself]
    earlier = (my_sources[None, :] == my_sources[:, None]) & (before.T > 0)
    offset = jnp.sum(jnp.where(earlier, my_tiles[None, :], 0), axis=1)
    shifted = tile_step[None, :] + my_shifts[:, None]
    inside = (shifted >= 0) & (shifted < tile_cols) & live_all[myself][:, None]
    slots = (
        my_sources[:, None] * capacity
        + offset[:, None]
        + tile_step[None, :]
        - jnp.maximum(-my_shifts, 0)[:, None]
    )
    slots = jnp.where(inside, slots, 0)
    per_tile = lambda x: x.reshape(vehicles_here, agents, tile_cols).transpose(0, 2, 1).reshape(-1, agents)
    bev_halo = row_halo(bev_maps)
    joined = agent_stage(bev_maps, arrived, per_tile(slots), per_tile(inside.astype(jnp.int32)),
                         agent_query, agent_keyvalue, agent_out, agent_scale)
    joined_halo = row_halo(joined)
    return layer_stage(bev_maps, joined, bev_halo, joined_halo, conv_weight, gain_first, window_in,
                       window_out, window_scale, gain_second, hidden_up, hidden_down)


def solution(mesh):
    split = P("veh", "row", None, None)
    return jax.shard_map(
        on_device, mesh=mesh, in_specs=(split,) + (P(),) * 15, out_specs=split, check_vma=False
    )
```

time: 579 us -> 318 us (0.55)
  matrix products: 148 us -> 0.19 us
  local copies, waits for them, and re-layouts: 156 us -> 10.1 us
  Pallas kernels: 0 us -> 103 us
  other arithmetic: 48 us -> 1.08 us
  loops' own time: 14.1 us -> 0 us
  waiting for transfers between devices: 185 us -> 177 us
    dot_general x70 -> x1, matrix products: 148 us -> 0.19 us  [on_device(): slot_start = jnp.dot(outgoing.astype(f32), before).astype(jnp.int32)]
    pallas_call x0 -> x3, Pallas kernels: none -> 103 us  [the longest x1 64.6 us: layer_stage(): pl.pallas_call(layer_kernel, grid=(vehicles,), in_specs=[block, block, ed...]
    reshape x16 -> x2, local copies, waits for them, and re-layouts: 40.8 us -> 1.27 us  [the longest x1 0.66 us: on_device(): jnp.sum(jnp.where(hit, base[:, None, :] + step, 0), axis=2).reshape(-1)]
    gather x5 -> x0, local copies, waits for them, and re-layouts: 39.2 us -> none  [the longest x4 26.5 us: agent_group(): sent_keyvalue = arrived[group_slots[:, None, :], band_rows]]
    convert_element_type x12 -> x1, local copies, waits for them, and re-layouts: 35.8 us -> 0.6 us  [on_device(): inside.astype(jnp.int32)]
    reduce_sum x20 -> x1, other arithmetic: 16.9 us -> 0.04 us  [on_device(): jnp.sum(jnp.where(hit, base[:, None, :] + step, 0), axis=2).reshape(-1)]
    scatter x1 -> x0, local copies, waits for them, and re-layouts: 15.5 us -> none  [on_device(): slot_table = jnp.full((devices * capacity,), -1, jnp.int32).at[target.res...]
    another operation x2 -> x0, loops' own time: 14.1 us -> none  [the longest x1 13.3 us: on_device(): lax.map(layer_group, padded.reshape(block_count, group_size, height + 2,...]
  transfers between devices with their start and end apart: 3 -> 5, of which waited for: 3 -> 2; matrix products, arithmetic and copies ran while one was open for 1% -> 2% of each run, Pallas kernels for 0% -> 9%
where the time goes in v1:
time: 318 us; the launch traced here: 314 us
  waiting for transfers between devices  177 us (56%)
  Pallas kernels  103 us (32%)
  starting transfers between devices  22.3 us (7%)
  local copies, waits for them, and re-layouts  10.1 us (3%)
    all_to_all x1, waiting for transfers between devices, on_device(): lax.all_to_all(packed, 'veh', split_axis=0, concat_axis=0, tiled=True)  174 us
    pallas_call x1, Pallas kernels, layer_stage(): pl.pallas_call(layer_kernel, grid=(vehicles,), in_specs=[block, block, ed...  64.6 us
    pallas_call x1, Pallas kernels, agent_stage(): pl.pallas_call(agent_kernel, grid_spec=pltpu.PrefetchScalarGridSpec(num_s...  29.5 us
    all_to_all x1, starting transfers between devices, on_device(): lax.all_to_all(packed, 'veh', split_axis=0, concat_axis=0, tiled=True)  13.5 us
    pallas_call x1, Pallas kernels, pack_tiles(): pl.pallas_call(pack_kernel, grid_spec=pltpu.PrefetchScalarGridSpec(num_sc...  8.98 us
  transfers between devices with their start and end apart: 5, of which 2 were waited for; matrix products, arithmetic and copies ran while one was open for 2% of the time, Pallas kernels for 9%

profile of v1, /device:TPU:1, one launch (start us, length us, event | category | flops | bytes accessed | tf_op | source)
XLA Modules:
  0.0 313.5 jit_solution(4699942730834664678)
XLA Ops:
  0.0 0.8 copy.23
  1.0 0.8 copy.26
  2.0 0.8 lt.95
  3.0 0.2 convolution_convert_fusion
  3.5 0.7 reshape.277.pick_ref
  4.2 9.0 %pack_tiles.1 = bf16[128,8,32,128]{3,2,1,0:T(8,128)(2,1)} custom-call(s32[128]{0:T(128)} %reshape.277.pick_ref, bf16[8,8,64,128]{3,2,1,0:T(8,128)(2,1)} %bev_ref.1), custom_call_target="tpu_custom_call" | custom-call | tf_op jit(solution)/shard_map/pack_tiles/pallas_call | solution.py:221
  13.2 13.5 %all-to-all-start = ((bf16[64,2,8,32,128]{4,3,2,1,0:T(8,128)(2,1)}), bf16[64,2,8,32,128]{4,3,2,1,0:T(8,128)(2,1)}, u32[]{:S(2)}, u32[]{:S(2)}) async-start(bf16[64,2,8,32,128]{4,3,2,1,0:T(8,128)(2,1)} %bitcast.9), calls=%async_computation | async-start | bytes 16777216 | tf_op jit(solution)/shard_map/all_to_all | solution.py:268
  26.6 1.0 fusion.14
  27.6 3.1 collective-permute-start
  30.8 1.3 collective-permute-start.1
  32.7 0.6 reshape.282.slot_ref
  33.3 0.6 reshape.283.live_ref
  34.0 0.7 broadcast_in_dim_reshape.6.scale_ref
  34.7 0.7 compare_convert_fusion.member_ref
  35.4 173.5 %all-to-all-done = bf16[64,2,8,32,128]{4,3,2,1,0:T(8,128)(2,1)} async-done(((bf16[64,2,8,32,128]{4,3,2,1,0:T(8,128)(2,1)}), bf16[64,2,8,32,128]{4,3,2,1,0:T(8,128)(2,1)}, u32[]{:S(2)}, u32[]{:S(2)}) %all-to-all-start) | async-done | bytes 8388640 | tf_op jit(solution)/shard_map/all_to_all | solution.py:268
  208.9 29.5 %agent_stage.1.joined_ref = bf16[8,8,64,128]{3,2,1,0:T(8,128)(2,1)} custom-call(s32[64]{0:T(128)} %reshape.282.slot_ref, s32[64]{0:T(128)} %reshape.283.live_ref, bf16[8,8,64,128]{3,2,1,0:T(8,128)(2,1)} %bev_ref.1, bf16[128,8,32,128]{3,2,1,0:T(8,128)(2,1)} %bitcast.4.t0.t1.t2.t3, bf16[128,8,32,128]{3,2,1,0:T(8,128)(2,1)} %bitcast.4.t0.t1.t2.t3, ...), custom_call_target="tpu_custom_call" | custom-call | tf_op jit(solution)/shard_map/agent_stage/pallas_call | solution.py:79
  238.4 1.0 fusion.13
  239.4 3.1 collective-permute-start.2
  242.5 1.3 collective-permute-start.3
  243.8 0.6 reshape.280.conv_ref
  244.5 0.6 broadcast_in_dim_reshape.7.scale_ref
  245.2 3.0 collective-permute-done.3.joined_down
  248.2 0.6 copy-done.3
  248.9 64.6 %layer_stage.1 = bf16[8,8,64,256]{3,2,1,0:T(8,128)(2,1)} custom-call(bf16[8,8,64,128]{3,2,1,0:T(8,128)(2,1)} %bev_ref.1, bf16[8,8,64,128]{3,2,1,0:T(8,128)(2,1)} %agent_stage.1.joined_ref, bf16[8,1,64,128]{3,2,1,0:T(8,128)(2,1)} %copy-done, bf16[8,1,64,128]{3,2,1,0:T(8,128)(2,1)} %copy-done.1, bf16[8,1,64,128]{3,2,1,0:T(8,128)(2,1)} %copy-done.2, ...), custom_call_target="tpu_custom_call" | custom-call | tf_op jit(solution)/shard_map/layer_stage/pallas_call | solution.py:196
  (44 shorter events, 1.6 us)
Async XLA Ops:
  13.2 20.8 %copy-start.5 = (f32[4]{0:T(128)S(1)}, f32[4]{0:T(128)}, u32[]{:S(2)}) copy-start(f32[4]{0:T(128)} %param.23) | copy-start | bytes 52
  13.2 195.8 %all-to-all-start = ((bf16[64,2,8,32,128]{4,3,2,1,0:T(8,128)(2,1)}), bf16[64,2,8,32,128]{4,3,2,1,0:T(8,128)(2,1)}, u32[]{:S(2)}, u32[]{:S(2)}) async-start(bf16[64,2,8,32,128]{4,3,2,1,0:T(8,128)(2,1)} %bitcast.9), calls=%async_computation | async-start | bytes 16777216 | tf_op jit(solution)/shard_map/all_to_all | solution.py:268
  27.6 217.5 %collective-permute-start = (bf16[8,1,64,128]{3,2,1,0:T(8,128)(2,1)S(1)}, bf16[8,1,64,128]{3,2,1,0:T(8,128)(2,1)S(1)}, u32[]{:S(2)}, u32[]{:S(2)}) collective-permute-start(bf16[8,1,64,128]{3,2,1,0:T(8,128)(2,1)S(1)} %get-tuple-element.11), channel_id=1, source_target_pairs={{0,1},{1,2},{2,3},{4,5},{5,6},{6,7},{8,9},{9,10},{10,11},{12,13},{... | collective-permute-start | bytes 393224 | tf_op jit(solution)/shard_map/ppermute | solution.py:239
  30.8 214.4 %collective-permute-start.1 = (bf16[8,1,64,128]{3,2,1,0:T(8,128)(2,1)S(1)}, bf16[8,1,64,128]{3,2,1,0:T(8,128)(2,1)S(1)}, u32[]{:S(2)}, u32[]{:S(2)}) collective-permute-start(bf16[8,1,64,128]{3,2,1,0:T(8,128)(2,1)S(1)} %get-tuple-element.10), channel_id=1, source_target_pairs={{1,0},{2,1},{3,2},{5,4},{6,5},{7,6},{9,8},{10,9},{11,10},{13,12},{... | collective-permute-start | bytes 393224 | tf_op jit(solution)/shard_map/ppermute | solution.py:240
  208.9 34.9 %copy-start.4 = (f32[3,3,256]{2,1,0:T(4,128)S(1)}, f32[3,3,256]{2,1,0:T(4,128)}, u32[]{:S(2)}) copy-start(f32[3,3,256]{2,1,0:T(4,128)} %param.24) | copy-start | bytes 27652
  208.9 35.5 %copy-start.6 = (f32[8]{0:T(128)S(1)}, f32[8]{0:T(128)}, u32[]{:S(2)}) copy-start(f32[8]{0:T(128)} %param.28) | copy-start | bytes 100
  239.4 5.8 %collective-permute-start.2 = (bf16[8,1,64,128]{3,2,1,0:T(8,128)(2,1)S(1)}, bf16[8,1,64,128]{3,2,1,0:T(8,128)(2,1)S(1)}, u32[]{:S(2)}, u32[]{:S(2)}) collective-permute-start(bf16[8,1,64,128]{3,2,1,0:T(8,128)(2,1)S(1)} %get-tuple-element.9), channel_id=1, source_target_pairs={{0,1},{1,2},{2,3},{4,5},{5,6},{6,7},{8,9},{9,10},{10,11},{12,13},{... | collective-permute-start | bytes 393224 | tf_op jit(solution)/shard_map/ppermute | solution.py:239
  242.5 5.7 %collective-permute-start.3 = (bf16[8,1,64,128]{3,2,1,0:T(8,128)(2,1)S(1)}, bf16[8,1,64,128]{3,2,1,0:T(8,128)(2,1)S(1)}, u32[]{:S(2)}, u32[]{:S(2)}) collective-permute-start(bf16[8,1,64,128]{3,2,1,0:T(8,128)(2,1)S(1)} %get-tuple-element.8), channel_id=1, source_target_pairs={{1,0},{2,1},{3,2},{5,4},{6,5},{7,6},{9,8},{10,9},{11,10},{13,12},{... | collective-permute-start | bytes 393224 | tf_op jit(solution)/shard_map/ppermute | solution.py:240
  245.2 3.1 copy-start
  245.2 3.1 copy-start.1
  245.2 3.0 copy-start.2
  248.2 0.7 copy-start.3

commit v2 on v1

--- a/solution.py
+++ b/solution.py
@@ -206,30 +206,123 @@
     )(bev_maps, joined, *bev_halo, *joined_halo, *small)
 
 
-def pack_kernel(pick_ref, maps_ref, packed_ref):
-    count = packed_ref.shape[0]
-    base = pl.program_id(0) * count
-    for k in range(count):
-        pick = pick_ref[base + k]
-        col = pl.multiple_of((pick % 2) * TILE, TILE)
-        packed_ref[k] = maps_ref[pick // 2, :, pl.ds(col, TILE), :]
-
-
-def pack_tiles(bev_maps, picks, per_step=8):
+RING = 8
+PLANE = 8
+HOPS = (0, -1, 1, -2, 2, -3, 3, 4)
+PIECES = 4
+SLOTS = 2
+
+
+def exchange_kernel(vehicle_ref, tile_ref, maps_ref, arrived_ref, f1, f2, f3, b1, b2, b3, far, outbox, ring_send,
+                    ring_recv, plane_send, plane_recv, own_sem):
+    me = lax.axis_index("veh")
+    plane, seat = me // PLANE, me % PLANE
+    depth = maps_ref.shape[0] // PIECES
+    ahead = {"veh": lax.rem(plane + 1, RING) * PLANE + seat}
+    behind = {"veh": lax.rem(plane + RING - 1, RING) * PLANE + seat}
+    peers = [{"veh": plane * PLANE + lax.rem(seat + j, PLANE)} for j in range(PLANE)]
+
+    barrier = pltpu.get_barrier_semaphore()
+    for peer in (ahead, behind, *peers[1:]):
+        pl.semaphore_signal(barrier, inc=1, device_id=peer, device_id_type=pl.DeviceIdType.MESH)
+    pl.semaphore_wait(barrier, PLANE + 1)
+
+    blocks = (maps_ref, f1, b1, f2, b2, f3, b3, far)
+    started = []
+
+    def pass_on(source, block, piece, target):
+        span = pl.ds(piece * depth, depth)
+        copy = pltpu.make_async_remote_copy(
+            src_ref=blocks[source].at[span],
+            dst_ref=blocks[block].at[span],
+            send_sem=ring_send.at[block - 1, piece],
+            recv_sem=ring_recv.at[block - 1, piece],
+            device_id=target,
+            device_id_type=pl.DeviceIdType.MESH,
+        )
+        copy.start()
+        started.append(copy)
+
+    def arrival(block, piece):
+        span = pl.ds(piece * depth, depth)
+        ref = blocks[block].at[span]
+        pltpu.make_async_copy(ref, ref, ring_recv.at[block - 1, piece]).wait()
+
+    def hand_out(block):
+        held = blocks[block]
+
+        def fill(j, carry):
+            for slot in range(SLOTS):
+                at = (block * PLANE + j) * SLOTS + slot
+                outbox[block, j, slot] = held[vehicle_ref[at], :, tile_ref[at]]
+            return carry
+
+        lax.fori_loop(0, PLANE, fill, 0)
+        for j in range(1, PLANE):
+            pltpu.make_async_remote_copy(
+                src_ref=outbox.at[block, j],
+                dst_ref=arrived_ref.at[block, seat],
+                send_sem=plane_send.at[0],
+                recv_sem=plane_recv.at[0],
+                device_id=peers[j],
+                device_id_type=pl.DeviceIdType.MESH,
+            ).start()
+        pltpu.make_async_copy(outbox.at[block, 0], arrived_ref.at[block, seat], own_sem.at[block]).start()
+
+    for piece in range(PIECES):
+        pass_on(0, 1, piece, ahead)
+        pass_on(0, 2, piece, behind)
+    hand_out(0)
+    for step in range(1, RING // 2):
+        front, back = 2 * step - 1, 2 * step
+        for piece in range(PIECES):
+            arrival(front, piece)
+            if step < RING // 2 - 1:
+                pass_on(front, front + 2, piece, ahead)
+            elif piece < PIECES // 2:
+                pass_on(front, RING - 1, piece, ahead)
+            arrival(back, piece)
+            if step < RING // 2 - 1:
+                pass_on(back, back + 2, piece, behind)
+            elif piece >= PIECES // 2:
+                pass_on(back, RING - 1, piece, behind)
+        hand_out(front)
+        hand_out(back)
+    for piece in range(PIECES):
+        arrival(RING - 1, piece)
+    hand_out(RING - 1)
+    for copy in started:
+        copy.wait_send()
+    sent = outbox.at[pl.ds(0, PLANE - 1)]
+    pltpu.make_async_copy(sent, sent, plane_send.at[0]).wait()
+    got = arrived_ref.at[pl.ds(0, PLANE - 1)]
+    pltpu.make_async_copy(got, got, plane_recv.at[0]).wait()
+    for block in range(RING):
+        pltpu.make_async_copy(outbox.at[block, 0], arrived_ref.at[block, seat], own_sem.at[block]).wait()
+
+
+def exchange(bev_maps, picks):
     vehicles, height, width_cells, channels = bev_maps.shape
-    slots = picks.shape[0]
+    tile_cols = width_cells // TILE
+    tiled = bev_maps.reshape(vehicles, height, tile_cols, TILE, channels)
+    box = (RING, PLANE, SLOTS, height, TILE, channels)
     return pl.pallas_call(
-        pack_kernel,
-        grid_spec=pltpu.PrefetchScalarGridSpec(
-            num_scalar_prefetch=1,
-            grid=(slots // per_step,),
-            in_specs=[pl.BlockSpec(bev_maps.shape, lambda i, *_: (0, 0, 0, 0))],
-            out_specs=pl.BlockSpec((per_step, height, TILE, channels), lambda i, *_: (i, 0, 0, 0)),
-        ),
-        out_shape=jax.ShapeDtypeStruct((slots, height, TILE, channels), bf16),
-        compiler_params=pltpu.CompilerParams(dimension_semantics=("arbitrary",)),
-        name="pack_tiles",
-    )(picks, bev_maps)
+        exchange_kernel,
+        in_specs=[pl.BlockSpec(memory_space=pltpu.SMEM)] * 2 + [pl.BlockSpec(memory_space=pltpu.VMEM)],
+        out_specs=pl.BlockSpec(memory_space=pl.ANY),
+        out_shape=jax.ShapeDtypeStruct(box, bf16),
+        scratch_shapes=[pltpu.VMEM(tiled.shape, bf16)] * (RING - 1)
+        + [
+            pltpu.VMEM(box, bf16),
+            pltpu.SemaphoreType.DMA((RING - 1, PIECES)),
+            pltpu.SemaphoreType.DMA((RING - 1, PIECES)),
+            pltpu.SemaphoreType.DMA((1,)),
+            pltpu.SemaphoreType.DMA((1,)),
+            pltpu.SemaphoreType.DMA((RING,)),
+        ],
+        compiler_params=pltpu.CompilerParams(collective_id=0, has_side_effects=True),
+        name="exchange",
+    )(picks // tile_cols, picks % tile_cols, tiled)
 
 
 def row_halo(cells):
@@ -241,52 +334,60 @@
     )
 
 
+def route(senders, shifts, counts, vehicles_here, tile_cols):
+    agents = senders.shape[1]
+    devices = lax.axis_size("veh")
+    myself = lax.axis_index("veh")
+    plane, seat = myself // PLANE, myself % PLANE
+    pair_count = vehicles_here * agents
+    by_block = lambda x: lax.dynamic_slice_in_dim(x.reshape(devices, -1), plane * PLANE, PLANE, axis=0)
+    sender = by_block(senders)
+    shift = by_block(shifts)
+    live = jnp.arange(agents)[None, None, :] < by_block(counts)[:, :, None]
+    live = live.reshape(PLANE, pair_count)
+    tiles = jnp.where(live, tile_cols - jnp.abs(shift), 0)
+    source = sender // vehicles_here
+    ordinal = jnp.arange(pair_count)
+    earlier = ordinal[None, :, None] > ordinal[None, None, :]
+    same = source[:, :, None] == source[:, None, :]
+    start = jnp.sum(jnp.where(same & earlier, tiles[:, None, :], 0), axis=2)
+    base = (sender % vehicles_here) * tile_cols + jnp.maximum(shift, 0)
+
+    hops = jnp.asarray(HOPS, jnp.int32)
+    origin = (plane + hops + RING) % RING * PLANE + seat
+    order = (seat + jnp.arange(PLANE)) % PLANE
+    turn = (order[:, None] == jnp.arange(PLANE)[None, :]).astype(jnp.int32)
+    slot = jnp.arange(SLOTS)[None, None, :, None]
+    step = slot - start[None, :, None, :]
+    hit = (source[None, :, None, :] == origin[:, None, None, None]) & (step >= 0)
+    hit = hit & (step < tiles[None, :, None, :])
+    picks = jnp.sum(jnp.where(hit, base[None, :, None, :] + step, 0), axis=3)
+    picks = jnp.sum(turn[None, :, :, None] * picks[:, None, :, :], axis=2).reshape(-1)
+
+    mine = lambda x: lax.dynamic_index_in_dim(x, seat, axis=0, keepdims=False)
+    my_source, my_shift, my_start, my_live = mine(source), mine(shift), mine(start), mine(live)
+    away = (my_source // PLANE - plane + RING) % RING
+    rank = jnp.where(away > RING // 2, 2 * (RING - away) - 1, jnp.maximum(2 * away, 0))
+    rank = jnp.where(away == RING // 2, RING - 1, rank)
+    tile_step = jnp.arange(tile_cols, dtype=jnp.int32)
+    shifted = tile_step[None, :] + my_shift[:, None]
+    inside = (shifted >= 0) & (shifted < tile_cols) & my_live[:, None]
+    slots = ((rank * PLANE + my_source % PLANE) * SLOTS + my_start)[:, None] + tile_step[None, :]
+    slots = slots - jnp.maximum(-my_shift, 0)[:, None]
+    slots = jnp.where(inside, slots, 0)
+    per_tile = lambda x: x.reshape(vehicles_here, agents, tile_cols).transpose(0, 2, 1).reshape(-1, agents)
+    return picks, per_tile(slots), per_tile(inside.astype(jnp.int32))
+
+
 def on_device(bev_maps, senders, shifts, counts, agent_query, agent_keyvalue, agent_out, agent_scale,
               conv_weight, gain_first, window_in, window_out, window_scale, gain_second, hidden_up,
               hidden_down):
     vehicles_here, height, width_cells, channels = bev_maps.shape
-    agents = senders.shape[1]
-    devices = lax.axis_size("veh")
-    myself = lax.axis_index("veh")
-    tile_cols = width_cells // TILE
-    pair_count = vehicles_here * agents
-    capacity = 2
-    send_all = senders.reshape(devices, pair_count)
-    shift_all = shifts.reshape(devices, pair_count)
-    live_all = (jnp.arange(agents)[None, :] < counts[:, None]).reshape(devices, pair_count)
-    tiles_all = jnp.where(live_all, tile_cols - jnp.abs(shift_all), 0)
-    source_all = send_all // vehicles_here
-    outgoing = jnp.where(source_all == myself, tiles_all, 0)
-    before = (jnp.arange(pair_count)[:, None] < jnp.arange(pair_count)[None, :]).astype(f32)
-    slot_start = jnp.dot(outgoing.astype(f32), before).astype(jnp.int32)
-    base = (send_all % vehicles_here) * tile_cols + jnp.maximum(shift_all, 0)
-    slot = jnp.arange(capacity)[None, :, None]
-    step = slot - slot_start[:, None, :]
-    hit = (step >= 0) & (step < outgoing[:, None, :])
-    picks = jnp.sum(jnp.where(hit, base[:, None, :] + step, 0), axis=2).reshape(-1)
-    packed = pack_tiles(bev_maps, picks).reshape(devices, capacity, height, TILE, channels)
-    arrived = lax.all_to_all(packed, "veh", split_axis=0, concat_axis=0, tiled=True)
-    arrived = arrived.reshape(devices * capacity, height, TILE, channels)
-
-    tile_step = jnp.arange(tile_cols, dtype=jnp.int32)
-    my_sources = source_all[myself]
-    my_shifts = shift_all[myself]
-    my_tiles = tiles_all[myself]
-    earlier = (my_sources[None, :] == my_sources[:, None]) & (before.T > 0)
-    offset = jnp.sum(jnp.where(earlier, my_tiles[None, :], 0), axis=1)
-    shifted = tile_step[None, :] + my_shifts[:, None]
-    inside = (shifted >= 0) & (shifted < tile_cols) & live_all[myself][:, None]
-    slots = (
-        my_sources[:, None] * capacity
-        + offset[:, None]
-        + tile_step[None, :]
-        - jnp.maximum(-my_shifts, 0)[:, None]
-    )
-    slots = jnp.where(inside, slots, 0)
-    per_tile = lambda x: x.reshape(vehicles_here, agents, tile_cols).transpose(0, 2, 1).reshape(-1, agents)
+    picks, slots, live = route(senders, shifts, counts, vehicles_here, width_cells // TILE)
+    arrived = exchange(bev_maps, picks).reshape(-1, height, TILE, channels)
     bev_halo = row_halo(bev_maps)
-    joined = agent_stage(bev_maps, arrived, per_tile(slots), per_tile(inside.astype(jnp.int32)),
-                         agent_query, agent_keyvalue, agent_out, agent_scale)
+    joined = agent_stage(bev_maps, arrived, slots, live, agent_query, agent_keyvalue, agent_out,
+                         agent_scale)
     joined_halo = row_halo(joined)
     return layer_stage(bev_maps, joined, bev_halo, joined_halo, conv_weight, gain_first, window_in,
                        window_out, window_scale, gain_second, hidden_up, hidden_down)

time: 318 us -> 238 us (0.75); the launches traced: 314 us -> 237 us
  waiting for transfers between devices: 177 us -> 4.19 us
  Pallas kernels: 103 us -> 210 us
  starting transfers between devices: 22.3 us -> 9.7 us
    all_to_all x1 -> x0, waiting for transfers between devices: 174 us -> none  [on_device(): lax.all_to_all(packed, 'veh', split_axis=0, concat_axis=0, tiled=True)]
    pallas_call x1, Pallas kernels: 8.98 us -> 116 us  [exchange(): pl.pallas_call(exchange_kernel, in_specs=[pl.BlockSpec(memory_space=pltpu...]
    all_to_all x1 -> x0, starting transfers between devices: 13.5 us -> none  [on_device(): lax.all_to_all(packed, 'veh', split_axis=0, concat_axis=0, tiled=True)]
  transfers between devices with their start and end apart: 5 -> 4, of which waited for: 2 -> 2; matrix products, arithmetic and copies ran while one was open for 2% -> 1% of each run, Pallas kernels for 9% -> 0%
where the time goes in v2:
time: 238 us; the launch traced here: 237 us
  Pallas kernels  210 us (88%)
  local copies, waits for them, and re-layouts  10.1 us (4%)
  starting transfers between devices  9.7 us (4%)
  waiting for transfers between devices  4.19 us (2%)
  other arithmetic  3.25 us (1%)
    pallas_call x1, Pallas kernels, exchange(): pl.pallas_call(exchange_kernel, in_specs=[pl.BlockSpec(memory_space=pltpu...  116 us
    pallas_call x1, Pallas kernels, layer_stage(): pl.pallas_call(layer_kernel, grid=(vehicles,), in_specs=[block, block, ed...  64.6 us
    pallas_call x1, Pallas kernels, agent_stage(): pl.pallas_call(agent_kernel, grid_spec=pltpu.PrefetchScalarGridSpec(num_s...  29.3 us
    ppermute x2, starting transfers between devices, row_halo(): lax.ppermute(cells[:, height - 1:], 'row', [(i, i + 1) for i in range(cou...  7.12 us
  transfers between devices with their start and end apart: 4, of which 2 were waited for; matrix products, arithmetic and copies ran while one was open for 1% of the time, Pallas kernels for 0%

profile of v2, /device:TPU:1, one launch (start us, length us, event | category | flops | bytes accessed | tf_op | source)
XLA Modules:
  0.0 237.4 jit_solution(7715040746605924175)
XLA Ops:
  0.0 0.8 reshape.345
  1.0 0.8 copy.22
  2.0 0.8 copy.25
  3.5 0.7 and_select_fusion.6
  4.7 0.4 multiply_reduce_fusion
  5.3 0.5 and_select_fusion.3
  6.1 0.7 reshape.353.live_ref
  7.0 0.6 reshape.352.slot_ref
  7.6 0.7 broadcast_in_dim.41
  8.3 0.6 broadcast_in_dim_reshape.6.scale_ref
  8.9 0.7 compare_convert_fusion.member_ref
  9.6 115.9 %exchange.1 = bf16[8,8,2,8,32,128]{5,4,3,2,1,0:T(8,128)(2,1)} custom-call(s32[128]{0:T(128)} %get-tuple-element.18.vehicle_ref, s32[128]{0:T(128)} %get-tuple-element.17.tile_ref, bf16[8,8,2,32,128]{4,3,2,1,0:T(8,128)(2,1)} %bitcast.9), custom_call_target="tpu_custom_call" | custom-call | tf_op jit(solution)/shard_map/exchange/pallas_call | solution.py:309
  125.6 29.3 %agent_stage.1.joined_ref = bf16[8,8,64,128]{3,2,1,0:T(8,128)(2,1)} custom-call(s32[64]{0:T(128)} %reshape.352.slot_ref, s32[64]{0:T(128)} %reshape.353.live_ref, bf16[8,8,64,128]{3,2,1,0:T(8,128)(2,1)} %bev_ref.1, bf16[128,8,32,128]{3,2,1,0:T(8,128)(2,1)} %bitcast.5, bf16[128,8,32,128]{3,2,1,0:T(8,128)(2,1)} %bitcast.6, bf16[128,8,32,128]{3,2,1,0:T(8,128)(2,1)} %bitcast.7, ...), custom_call_target="tpu_custom_call" | custom-call | tf_op jit(solution)/shard_map/agent_stage/pallas_call | solution.py:79
  154.9 1.0 fusion.24
  155.9 3.1 %collective-permute-start.2 = (bf16[8,1,64,128]{3,2,1,0:T(8,128)(2,1)S(1)}, bf16[8,1,64,128]{3,2,1,0:T(8,128)(2,1)S(1)}, u32[]{:S(2)}, u32[]{:S(2)}) collective-permute-start(bf16[8,1,64,128]{3,2,1,0:T(8,128)(2,1)S(1)} %get-tuple-element.10), channel_id=1, source_target_pairs={{0,1},{1,2},{2,3},{4,5},{5,6},{6,7},{8,9},{9,10},{10,11},{12,13},{... | collective-permute-start | bytes 393224 | tf_op jit(solution)/shard_map/ppermute | solution.py:332
  159.1 1.3 collective-permute-start.3
  160.4 1.0 fusion.25
  161.4 4.0 %collective-permute-start = (bf16[8,1,64,128]{3,2,1,0:T(8,128)(2,1)S(1)}, bf16[8,1,64,128]{3,2,1,0:T(8,128)(2,1)S(1)}, u32[]{:S(2)}, u32[]{:S(2)}) collective-permute-start(bf16[8,1,64,128]{3,2,1,0:T(8,128)(2,1)S(1)} %get-tuple-element.12), channel_id=1, source_target_pairs={{0,1},{1,2},{2,3},{4,5},{5,6},{6,7},{8,9},{9,10},{10,11},{12,13},{... | collective-permute-start | bytes 393224 | tf_op jit(solution)/shard_map/ppermute | solution.py:332
  165.4 1.3 collective-permute-start.1
  166.7 0.6 reshape.350.conv_ref
  167.3 0.6 broadcast_in_dim_reshape.7.scale_ref
  168.3 3.8 %collective-permute-done.1.bev_down = bf16[8,1,64,128]{3,2,1,0:T(8,128)(2,1)S(1)} collective-permute-done((bf16[8,1,64,128]{3,2,1,0:T(8,128)(2,1)S(1)}, bf16[8,1,64,128]{3,2,1,0:T(8,128)(2,1)S(1)}, u32[]{:S(2)}, u32[]{:S(2)}) %collective-permute-start.1) | collective-permute-done | bytes 131104 | tf_op jit(solution)/shard_map/ppermute | solution.py:333
  172.2 0.6 copy-done.3
  172.8 64.6 %layer_stage.1 = bf16[8,8,64,256]{3,2,1,0:T(8,128)(2,1)} custom-call(bf16[8,8,64,128]{3,2,1,0:T(8,128)(2,1)} %bev_ref.1, bf16[8,8,64,128]{3,2,1,0:T(8,128)(2,1)} %agent_stage.1.joined_ref, bf16[8,1,64,128]{3,2,1,0:T(8,128)(2,1)} %copy-done.2, bf16[8,1,64,128]{3,2,1,0:T(8,128)(2,1)} %copy-done.3, bf16[8,1,64,128]{3,2,1,0:T(8,128)(2,1)} %copy-done, ...), custom_call_target="tpu_custom_call" | custom-call | tf_op jit(solution)/shard_map/layer_stage/pallas_call | solution.py:196
  (47 shorter events, 2.6 us)
Async XLA Ops:
  125.6 41.1 %copy-start.4 = (f32[3,3,256]{2,1,0:T(4,128)S(1)}, f32[3,3,256]{2,1,0:T(4,128)}, u32[]{:S(2)}) copy-start(f32[3,3,256]{2,1,0:T(4,128)} %param.25) | copy-start | bytes 27652
  125.6 41.7 %copy-start.5 = (f32[8]{0:T(128)S(1)}, f32[8]{0:T(128)}, u32[]{:S(2)}) copy-start(f32[8]{0:T(128)} %param.29) | copy-start | bytes 100
  155.9 12.0 %collective-permute-start.2 = (bf16[8,1,64,128]{3,2,1,0:T(8,128)(2,1)S(1)}, bf16[8,1,64,128]{3,2,1,0:T(8,128)(2,1)S(1)}, u32[]{:S(2)}, u32[]{:S(2)}) collective-permute-start(bf16[8,1,64,128]{3,2,1,0:T(8,128)(2,1)S(1)} %get-tuple-element.10), channel_id=1, source_target_pairs={{0,1},{1,2},{2,3},{4,5},{5,6},{6,7},{8,9},{9,10},{10,11},{12,13},{... | collective-permute-start | bytes 393224 | tf_op jit(solution)/shard_map/ppermute | solution.py:332
  159.1 8.9 %collective-permute-start.3 = (bf16[8,1,64,128]{3,2,1,0:T(8,128)(2,1)S(1)}, bf16[8,1,64,128]{3,2,1,0:T(8,128)(2,1)S(1)}, u32[]{:S(2)}, u32[]{:S(2)}) collective-permute-start(bf16[8,1,64,128]{3,2,1,0:T(8,128)(2,1)S(1)} %get-tuple-element.9), channel_id=1, source_target_pairs={{1,0},{2,1},{3,2},{5,4},{6,5},{7,6},{9,8},{10,9},{11,10},{13,12},{... | collective-permute-start | bytes 393224 | tf_op jit(solution)/shard_map/ppermute | solution.py:333
  161.4 7.0 %collective-permute-start = (bf16[8,1,64,128]{3,2,1,0:T(8,128)(2,1)S(1)}, bf16[8,1,64,128]{3,2,1,0:T(8,128)(2,1)S(1)}, u32[]{:S(2)}, u32[]{:S(2)}) collective-permute-start(bf16[8,1,64,128]{3,2,1,0:T(8,128)(2,1)S(1)} %get-tuple-element.12), channel_id=1, source_target_pairs={{0,1},{1,2},{2,3},{4,5},{5,6},{6,7},{8,9},{9,10},{10,11},{12,13},{... | collective-permute-start | bytes 393224 | tf_op jit(solution)/shard_map/ppermute | solution.py:332
  165.4 6.8 %collective-permute-start.1 = (bf16[8,1,64,128]{3,2,1,0:T(8,128)(2,1)S(1)}, bf16[8,1,64,128]{3,2,1,0:T(8,128)(2,1)S(1)}, u32[]{:S(2)}, u32[]{:S(2)}) collective-permute-start(bf16[8,1,64,128]{3,2,1,0:T(8,128)(2,1)S(1)} %get-tuple-element.11), channel_id=1, source_target_pairs={{1,0},{2,1},{3,2},{5,4},{6,5},{7,6},{9,8},{10,9},{11,10},{13,12},{... | collective-permute-start | bytes 393224 | tf_op jit(solution)/shard_map/ppermute | solution.py:333
  168.0 4.2 %copy-start = (bf16[8,1,64,128]{3,2,1,0:T(8,128)(2,1)}, bf16[8,1,64,128]{3,2,1,0:T(8,128)(2,1)S(1)}, u32[]{:S(2)}) copy-start(bf16[8,1,64,128]{3,2,1,0:T(8,128)(2,1)S(1)} %collective-permute-done.2.joined_up) | copy-start | bytes 393220
  168.0 4.2 %copy-start.1 = (bf16[8,1,64,128]{3,2,1,0:T(8,128)(2,1)}, bf16[8,1,64,128]{3,2,1,0:T(8,128)(2,1)S(1)}, u32[]{:S(2)}) copy-start(bf16[8,1,64,128]{3,2,1,0:T(8,128)(2,1)S(1)} %collective-permute-done.3.joined_down) | copy-start | bytes 393220
  168.3 3.8 %copy-start.2 = (bf16[8,1,64,128]{3,2,1,0:T(8,128)(2,1)}, bf16[8,1,64,128]{3,2,1,0:T(8,128)(2,1)S(1)}, u32[]{:S(2)}) copy-start(bf16[8,1,64,128]{3,2,1,0:T(8,128)(2,1)S(1)} %collective-permute-done.bev_up) | copy-start | bytes 393220
  172.2 0.7 copy-start.3

commit v3 on v2

--- a/solution.py
+++ b/solution.py
@@ -29,25 +29,26 @@
 
 
 def agent_kernel(slot_ref, live_ref, ego_ref, t0, t1, t2, t3, query_ref, keyvalue_ref, out_w_ref,
-                 scale_ref, member_ref, joined_ref):
+                 scale_ref, joined_ref):
     step = pl.program_id(0)
     tiles = (t0, t1, t2, t3)
     height, cols, channels = ego_ref.shape[1:]
     cells = height * cols
     ego = ego_ref[0].reshape(cells, channels)
-    member = member_ref[...]
+    member = member_matrix(channels)
     query = jnp.dot(ego, query_ref[...], preferred_element_type=f32)
-    query = query * (lax.rsqrt(head_sums(query * query, member) + unit_eps) * scale_ref[...])
-    scores, values = [], []
-    for a in range(len(tiles) + 1):
-        source = ego if a == 0 else tiles[a - 1][0].reshape(cells, channels)
-        keyvalue = jnp.dot(source, keyvalue_ref[...], preferred_element_type=f32).astype(bf16)
-        key = keyvalue[:, :channels].astype(f32)
-        values.append(keyvalue[:, channels:])
-        score = head_sums(query * key, member) * lax.rsqrt(head_sums(key * key, member) + unit_eps)
-        if a:
-            score = score + jnp.where(live_ref[step * len(tiles) + a - 1] > 0, 0.0, -1e30)
-        scores.append(score)
+    count = len(tiles) + 1
+    sources = jnp.concatenate([ego] + [t[0].reshape(cells, channels) for t in tiles], axis=0)
+    keyvalue = jnp.dot(sources, keyvalue_ref[...], preferred_element_type=f32).astype(bf16)
+    query = query * (lax.rsqrt(head_sums(query * query, member) + unit_eps) * scale_row(scale_ref, 0, channels))
+    key = keyvalue[:, :channels].astype(f32)
+    norms = head_sums(key * key, member)
+    products = head_sums((key.reshape(count, cells, channels) * query[None]).reshape(count * cells, channels), member)
+    score = products * lax.rsqrt(norms + unit_eps)
+    scores = [score[a * cells : (a + 1) * cells] for a in range(count)]
+    values = [keyvalue[a * cells : (a + 1) * cells, channels:] for a in range(count)]
+    for a in range(len(tiles)):
+        scores[a + 1] = scores[a + 1] + jnp.where(live_ref[step * len(tiles) + a] > 0, 0.0, -1e30)
     top = functools.reduce(jnp.maximum, scores)
     total, mix = None, None
     for score, value in zip(scores, values):
@@ -61,8 +62,17 @@
 
 
 def member_matrix(width):
-    rows = jnp.arange(2 * width)[:, None] % width // HEAD
-    return (rows == jnp.arange(width)[None, :] // HEAD).astype(bf16)
+    rows = lax.broadcasted_iota(jnp.int32, (2 * width, width), 0) % width // HEAD
+    lanes = lax.broadcasted_iota(jnp.int32, (2 * width, width), 1) // HEAD
+    return jnp.where(rows == lanes, 1.0, 0.0).astype(bf16)
+
+
+def scale_row(scale_ref, first, width):
+    head = lax.broadcasted_iota(jnp.int32, (1, width), 1) // HEAD
+    row = jnp.full((1, width), scale_ref[first], f32)
+    for j in range(1, width // HEAD):
+        row = jnp.where(head == j, scale_ref[first + j], row)
+    return row
 
 
 def agent_stage(bev_maps, arrived, slots, live, agent_query, agent_keyvalue, agent_out, agent_scale):
@@ -75,7 +85,6 @@
         pl.BlockSpec((1, height, TILE, channels), lambda i, s, l, a=a: (s[i * agents + a], 0, 0, 0))
         for a in range(agents)
     ]
-    scale_row = jnp.repeat(agent_scale, channels // agent_scale.shape[0])[None]
     return pl.pallas_call(
         agent_kernel,
         grid_spec=pltpu.PrefetchScalarGridSpec(
@@ -83,14 +92,14 @@
             grid=(vehicles * tile_cols,),
             in_specs=[ego_spec, *tile_specs]
             + [pl.BlockSpec(w.shape, full) for w in (agent_query, agent_keyvalue, agent_out)]
-            + [pl.BlockSpec((1, channels), full), pl.BlockSpec((2 * channels, channels), full)],
+            + [pl.BlockSpec(memory_space=pltpu.SMEM)],
             out_specs=ego_spec,
         ),
         out_shape=jax.ShapeDtypeStruct(bev_maps.shape, bf16),
         compiler_params=pltpu.CompilerParams(dimension_semantics=("arbitrary",)),
         name="agent_stage",
     )(slots.reshape(-1), live.reshape(-1), bev_maps, arrived, arrived, arrived, arrived, agent_query,
-      agent_keyvalue, agent_out, scale_row, member_matrix(channels))
+      agent_keyvalue, agent_out, agent_scale)
 
 
 def layer_norm(x, gain):
@@ -100,7 +109,7 @@
 
 
 def layer_kernel(bev_ref, joined_ref, bev_up, bev_down, joined_up, joined_down, conv_ref, gain1_ref,
-                 in_ref, out_w_ref, scale_ref, gain2_ref, up_ref, down_ref, member_ref, out_ref,
+                 in_ref, out_w_ref, scale_ref, gain2_ref, up_ref, down_ref, out_ref,
                  mixed_ref, attended_ref):
     height, cols, channels = bev_ref.shape[1:]
     cells = height * cols
@@ -108,14 +117,19 @@
     area = WIN * WIN
     width = 2 * channels
     column = lax.broadcasted_iota(jnp.int32, (cells, channels), 0) % cols
+    band = lax.axis_index("row")
+    has_up = jnp.where(band > 0, 1.0, 0.0)
+    has_down = jnp.where(band < lax.axis_size("row") - 1, 1.0, 0.0)
     for half, (main, top, bottom) in enumerate(
         ((bev_ref, bev_up, bev_down), (joined_ref, joined_up, joined_down))
     ):
         lanes = slice(half * channels, (half + 1) * channels)
-        rows = jnp.concatenate([top[0], main[0], bottom[0]], axis=0).astype(f32)
+        rows = jnp.concatenate(
+            [top[0].astype(f32) * has_up, main[0].astype(f32), bottom[0].astype(f32) * has_down], axis=0
+        )
         sums = []
         for dj in range(3):
-            taps = [conv_ref[di * 3 + dj : di * 3 + dj + 1, lanes] for di in range(3)]
+            taps = [conv_ref[di, dj : dj + 1, lanes] for di in range(3)]
             if dj == 1:
                 taps[1] = taps[1] + 1.0
             acc = rows[0:height] * taps[0] + rows[1 : height + 1] * taps[1] + rows[2:] * taps[2]
@@ -133,37 +147,47 @@
     mixed = mixed_ref[...]
     hidden = layer_norm(mixed, gain1_ref[...])
     projected = jnp.dot(hidden, in_ref[...], preferred_element_type=f32)
-    member = member_ref[...]
+    member = member_matrix(channels)
     groups = []
     for g in range(width // channels):
-        lanes = slice(g * channels, (g + 1) * channels)
         query = projected[:, g * channels : (g + 1) * channels]
         key = projected[:, width + g * channels : width + (g + 1) * channels]
-        query = query * (lax.rsqrt(head_sums(query * query, member) + unit_eps) * scale_ref[:, lanes])
+        query = query * (lax.rsqrt(head_sums(query * query, member) + unit_eps) * scale_row(scale_ref, g * (channels // HEAD), channels))
         key = key * lax.rsqrt(head_sums(key * key, member) + unit_eps)
         value = projected[:, 2 * width + g * channels : 2 * width + (g + 1) * channels].astype(bf16)
         groups.append((jnp.concatenate(halves(query), axis=-1), *halves(key), value))
     heads = channels // HEAD
     head_of = lax.broadcasted_iota(jnp.int32, (area, 2 * channels), 1) % channels // HEAD
     lane_head = lax.broadcasted_iota(jnp.int32, (area, channels), 1) // HEAD
-    for w in range(windows):
+    def score_of(w, g):
+        query, key_high, key_low, value = groups[g]
         span = slice(w * area, (w + 1) * area)
-        for g, (query, key_high, key_low, value) in enumerate(groups):
-            q = query[span]
-            spread_q = jnp.concatenate(
-                [jnp.where(head_of == j, q, jnp.zeros_like(q)) for j in range(heads)], axis=0
-            )
-            kh = key_high[span]
-            scores = nt_dot(jnp.concatenate([kh, kh], axis=-1), spread_q) + nt_dot(
-                key_low[span], spread_q[:, :channels]
-            )
-            weight = jnp.exp(scores - jnp.max(scores, axis=0, keepdims=True))
-            weight = weight * (1.0 / jnp.sum(weight, axis=0, keepdims=True))
-            mixed_values = jnp.dot(weight.T.astype(bf16), value[span], preferred_element_type=f32)
-            attended = jnp.where(lane_head == 0, mixed_values[:area], 0.0)
-            for j in range(1, heads):
-                attended = jnp.where(lane_head == j, mixed_values[j * area : (j + 1) * area], attended)
-            attended_ref[span, g * channels : (g + 1) * channels] = attended.astype(bf16)
+        q = query[span]
+        spread_q = jnp.concatenate(
+            [jnp.where(head_of == j, q, jnp.zeros_like(q)) for j in range(heads)], axis=0
+        )
+        kh = key_high[span]
+        return nt_dot(jnp.concatenate([kh, kh], axis=-1), spread_q) + nt_dot(
+            key_low[span], spread_q[:, :channels]
+        )
+
+    def soften(scores):
+        weight = jnp.exp(scores - jnp.max(scores, axis=0, keepdims=True))
+        return (weight * (1.0 / jnp.sum(weight, axis=0, keepdims=True))).astype(bf16)
+
+    def finish(w, g, weight):
+        span = slice(w * area, (w + 1) * area)
+        mixed_values = lax.dot_general(weight, groups[g][3][span], (((0,), (0,)), ((), ())), preferred_element_type=f32)
+        attended = mixed_values[:area]
+        for j in range(1, heads):
+            attended = jnp.where(lane_head == j, mixed_values[j * area : (j + 1) * area], attended)
+        attended_ref[span, g * channels : (g + 1) * channels] = attended.astype(bf16)
+
+    units = [(w, g) for w in range(windows) for g in range(len(groups))]
+    all_scores = [score_of(w, g) for w, g in units]
+    all_weights = [soften(s) for s in all_scores]
+    for (w, g), weight in zip(units, all_weights):
+        finish(w, g, weight)
     mixed = mixed + jnp.dot(attended_ref[...], out_w_ref[...], preferred_element_type=f32)
     hidden = layer_norm(mixed, gain2_ref[...])
     inner = jnp.dot(hidden, up_ref[...], preferred_element_type=f32)
@@ -182,22 +206,15 @@
     cells = height * width_cells
     block = pl.BlockSpec((1, height, width_cells, channels), lambda i: (i, 0, 0, 0))
     edge = pl.BlockSpec((1, 1, width_cells, channels), lambda i: (i, 0, 0, 0))
-    small = (
-        conv_weight.reshape(9, width),
-        gain_first[None],
-        window_in,
-        window_out,
-        jnp.repeat(window_scale, width // window_scale.shape[0])[None],
-        gain_second[None],
-        hidden_up,
-        hidden_down,
-        member_matrix(channels),
-    )
+    small = (conv_weight, gain_first[None], window_in, window_out, window_scale, gain_second[None],
+             hidden_up, hidden_down)
+    whole = lambda w: pl.BlockSpec(w.shape, lambda i: (0,) * w.ndim)
+    scalars = pl.BlockSpec(memory_space=pltpu.SMEM)
     return pl.pallas_call(
         layer_kernel,
         grid=(vehicles,),
         in_specs=[block, block, edge, edge, edge, edge]
-        + [pl.BlockSpec(w.shape, lambda i: (0, 0)) for w in small],
+        + [scalars if w is window_scale else whole(w) for w in small],
         out_specs=pl.BlockSpec((1, height, width_cells, width), lambda i: (i, 0, 0, 0)),
         out_shape=jax.ShapeDtypeStruct((vehicles, height, width_cells, width), bf16),
         scratch_shapes=[pltpu.VMEM((cells, width), f32), pltpu.VMEM((cells, width), bf16)],
@@ -209,32 +226,39 @@
 RING = 8
 PLANE = 8
 HOPS = (0, -1, 1, -2, 2, -3, 3, 4)
-PIECES = 4
+PIECES = 2
 SLOTS = 2
 
 
-def exchange_kernel(vehicle_ref, tile_ref, maps_ref, arrived_ref, f1, f2, f3, b1, b2, b3, far, outbox, ring_send,
-                    ring_recv, plane_send, plane_recv, own_sem):
+def exchange_kernel(vehicle_ref, tile_ref, maps_ref, arrived_ref, up_ref, down_ref, *scratch):
+    outbox, ring_send, ring_recv, plane_send, plane_recv, own_sem, edge_send, edge_recv = scratch[-8:]
     me = lax.axis_index("veh")
     plane, seat = me // PLANE, me % PLANE
-    depth = maps_ref.shape[0] // PIECES
+    height = maps_ref.shape[1]
+    bands = lax.axis_size("row")
+    band = lax.axis_index("row")
+    below = {"row": lax.rem(band + 1, bands)}
+    above = {"row": lax.rem(band + bands - 1, bands)}
     ahead = {"veh": lax.rem(plane + 1, RING) * PLANE + seat}
     behind = {"veh": lax.rem(plane + RING - 1, RING) * PLANE + seat}
     peers = [{"veh": plane * PLANE + lax.rem(seat + j, PLANE)} for j in range(PLANE)]
 
     barrier = pltpu.get_barrier_semaphore()
-    for peer in (ahead, behind, *peers[1:]):
+    for peer in (ahead, behind, below, above, *peers[1:]):
         pl.semaphore_signal(barrier, inc=1, device_id=peer, device_id_type=pl.DeviceIdType.MESH)
-    pl.semaphore_wait(barrier, PLANE + 1)
-
-    blocks = (maps_ref, f1, b1, f2, b2, f3, b3, far)
+    pl.semaphore_wait(barrier, PLANE + 3)
+
     started = []
 
+    def held(block, piece):
+        if block == 0:
+            return maps_ref.at[:, :, :, piece]
+        return scratch[(block - 1) * PIECES + piece]
+
     def pass_on(source, block, piece, target):
-        span = pl.ds(piece * depth, depth)
         copy = pltpu.make_async_remote_copy(
-            src_ref=blocks[source].at[span],
-            dst_ref=blocks[block].at[span],
+            src_ref=held(source, piece),
+            dst_ref=held(block, piece),
             send_sem=ring_send.at[block - 1, piece],
             recv_sem=ring_recv.at[block - 1, piece],
             device_id=target,
@@ -244,35 +268,46 @@
         started.append(copy)
 
     def arrival(block, piece):
-        span = pl.ds(piece * depth, depth)
-        ref = blocks[block].at[span]
+        ref = held(block, piece)
         pltpu.make_async_copy(ref, ref, ring_recv.at[block - 1, piece]).wait()
 
-    def hand_out(block):
-        held = blocks[block]
+    def hand_out(block, piece):
+        source = held(block, piece)
 
         def fill(j, carry):
             for slot in range(SLOTS):
                 at = (block * PLANE + j) * SLOTS + slot
-                outbox[block, j, slot] = held[vehicle_ref[at], :, tile_ref[at]]
+                outbox[block, j, slot, :, piece] = source[vehicle_ref[at], :, tile_ref[at]]
             return carry
 
         lax.fori_loop(0, PLANE, fill, 0)
         for j in range(1, PLANE):
             pltpu.make_async_remote_copy(
-                src_ref=outbox.at[block, j],
-                dst_ref=arrived_ref.at[block, seat],
+                src_ref=outbox.at[block, j, :, :, piece],
+                dst_ref=arrived_ref.at[block, seat, :, :, piece],
                 send_sem=plane_send.at[0],
                 recv_sem=plane_recv.at[0],
                 device_id=peers[j],
                 device_id_type=pl.DeviceIdType.MESH,
             ).start()
-        pltpu.make_async_copy(outbox.at[block, 0], arrived_ref.at[block, seat], own_sem.at[block]).start()
-
+
+    edges = []
+    for at, (row, ref, target) in enumerate(((height - 1, up_ref, below), (0, down_ref, above))):
+        edge = pltpu.make_async_remote_copy(
+            src_ref=maps_ref.at[:, row],
+            dst_ref=ref,
+            send_sem=edge_send.at[at],
+            recv_sem=edge_recv.at[at],
+            device_id=target,
+            device_id_type=pl.DeviceIdType.MESH,
+        )
+        edge.start()
+        edges.append(edge)
     for piece in range(PIECES):
         pass_on(0, 1, piece, ahead)
         pass_on(0, 2, piece, behind)
-    hand_out(0)
+    for piece in range(PIECES):
+        hand_out(0, piece)
     for step in range(1, RING // 2):
         front, back = 2 * step - 1, 2 * step
         for piece in range(PIECES):
@@ -286,11 +321,15 @@
                 pass_on(back, back + 2, piece, behind)
             elif piece >= PIECES // 2:
                 pass_on(back, RING - 1, piece, behind)
-        hand_out(front)
-        hand_out(back)
+            hand_out(front, piece)
+            hand_out(back, piece)
     for piece in range(PIECES):
         arrival(RING - 1, piece)
-    hand_out(RING - 1)
+        hand_out(RING - 1, piece)
+    for block in range(RING):
+        pltpu.make_async_copy(outbox.at[block, 0], arrived_ref.at[block, seat], own_sem.at[block]).start()
+    for edge in edges:
+        edge.wait()
     for copy in started:
         copy.wait_send()
     sent = outbox.at[pl.ds(0, PLANE - 1)]
@@ -304,14 +343,17 @@
 def exchange(bev_maps, picks):
     vehicles, height, width_cells, channels = bev_maps.shape
     tile_cols = width_cells // TILE
-    tiled = bev_maps.reshape(vehicles, height, tile_cols, TILE, channels)
-    box = (RING, PLANE, SLOTS, height, TILE, channels)
-    return pl.pallas_call(
+    part = TILE // PIECES
+    tiled = bev_maps.reshape(vehicles, height, tile_cols, PIECES, part, channels)
+    box = (RING, PLANE, SLOTS, height, PIECES, part, channels)
+    edge = (vehicles,) + tiled.shape[2:]
+    shapes = (box, edge, edge)
+    arrived, up, down = pl.pallas_call(
         exchange_kernel,
         in_specs=[pl.BlockSpec(memory_space=pltpu.SMEM)] * 2 + [pl.BlockSpec(memory_space=pltpu.VMEM)],
-        out_specs=pl.BlockSpec(memory_space=pl.ANY),
-        out_shape=jax.ShapeDtypeStruct(box, bf16),
-        scratch_shapes=[pltpu.VMEM(tiled.shape, bf16)] * (RING - 1)
+        out_specs=[pl.BlockSpec(memory_space=pl.ANY)] * 3,
+        out_shape=[jax.ShapeDtypeStruct(s, bf16) for s in shapes],
+        scratch_shapes=[pltpu.VMEM(tiled.shape[:3] + tiled.shape[4:], bf16)] * ((RING - 1) * PIECES)
         + [
             pltpu.VMEM(box, bf16),
             pltpu.SemaphoreType.DMA((RING - 1, PIECES)),
@@ -319,10 +361,14 @@
             pltpu.SemaphoreType.DMA((1,)),
             pltpu.SemaphoreType.DMA((1,)),
             pltpu.SemaphoreType.DMA((RING,)),
+            pltpu.SemaphoreType.DMA((2,)),
+            pltpu.SemaphoreType.DMA((2,)),
         ],
         compiler_params=pltpu.CompilerParams(collective_id=0, has_side_effects=True),
         name="exchange",
     )(picks // tile_cols, picks % tile_cols, tiled)
+    flat = (vehicles, 1, width_cells, channels)
+    return arrived.reshape(-1, height, TILE, channels), (up.reshape(flat), down.reshape(flat))
 
 
 def row_halo(cells):
@@ -384,8 +430,7 @@
               hidden_down):
     vehicles_here, height, width_cells, channels = bev_maps.shape
     picks, slots, live = route(senders, shifts, counts, vehicles_here, width_cells // TILE)
-    arrived = exchange(bev_maps, picks).reshape(-1, height, TILE, channels)
-    bev_halo = row_halo(bev_maps)
+    arrived, bev_halo = exchange(bev_maps, picks)
     joined = agent_stage(bev_maps, arrived, slots, live, agent_query, agent_keyvalue, agent_out,
                          agent_scale)
     joined_halo = row_halo(joined)

time: 238 us -> 173 us (0.73)
  Pallas kernels: 210 us -> 155 us
  starting transfers between devices: 9.7 us -> 5.29 us
  local copies, waits for them, and re-layouts: 10.1 us -> 6.51 us
    pallas_call x1, Pallas kernels: 64.6 us -> 29.2 us  [layer_stage(): pl.pallas_call(layer_kernel, grid=(vehicles,), in_specs=[block, block, ed...]
    pallas_call x1, Pallas kernels: 116 us -> 105 us  [exchange(): pl.pallas_call(exchange_kernel, in_specs=[pl.BlockSpec(memory_space=pltpu...]
    pallas_call x1, Pallas kernels: 29.3 us -> 20.4 us  [agent_stage(): pl.pallas_call(agent_kernel, grid_spec=pltpu.PrefetchScalarGridSpec(num_s...]
    ppermute x2 -> x1, starting transfers between devices: 7.12 us -> 3.99 us  [row_halo(): lax.ppermute(cells[:, height - 1:], 'row', [(i, i + 1) for i in range(cou...]
  transfers between devices with their start and end apart: 4 -> 2, of which waited for: 2 -> 2; matrix products, arithmetic and copies ran while one was open for 1% -> 0% of each run, Pallas kernels for 0% -> 0%
where the time goes in v3:
time: 173 us; the launch traced here: 172 us
  Pallas kernels  155 us (90%)
  local copies, waits for them, and re-layouts  6.51 us (4%)
  starting transfers between devices  5.29 us (3%)
  waiting for transfers between devices  2.55 us (1%)
  other arithmetic  2.51 us (1%)
    pallas_call x1, Pallas kernels, exchange(): pl.pallas_call(exchange_kernel, in_specs=[pl.BlockSpec(memory_space=pltpu...  105 us
    pallas_call x1, Pallas kernels, layer_stage(): pl.pallas_call(layer_kernel, grid=(vehicles,), in_specs=[block, block, ed...  29.2 us
    pallas_call x1, Pallas kernels, agent_stage(): pl.pallas_call(agent_kernel, grid_spec=pltpu.PrefetchScalarGridSpec(num_s...  20.4 us
    ppermute x1, starting transfers between devices, row_halo(): lax.ppermute(cells[:, height - 1:], 'row', [(i, i + 1) for i in range(cou...  3.99 us
  transfers between devices with their start and end apart: 2, of which 2 were waited for; matrix products, arithmetic and copies ran while one was open for 0% of the time, Pallas kernels for 0%

profile of v3, /device:TPU:1, one launch (start us, length us, event | category | flops | bytes accessed | tf_op | source)
XLA Modules:
  0.0 171.8 jit_solution(14020347361276883469)
XLA Ops:
  0.1 0.8 reshape.263
  1.1 0.8 copy.25
  1.9 0.1 reshape.264
  2.1 0.8 copy.22
  2.9 0.1 reshape.262
  3.1 0.3 select_reduce_fusion
  3.4 0.7 and_select_fusion.3
  4.2 0.1 and.144
  4.7 0.6 reshape.271.slot_ref
  5.3 0.7 reshape.272.live_ref
  6.0 0.4 select_reduce_fusion.1
  6.4 0.4 multiply_reduce_fusion
  6.8 0.1 copy.26
  6.9 0.1 reshape.265
  7.0 0.5 and_select_fusion
  7.6 105.1 %exchange.1 = (bf16[8,8,2,8,2,16,128]{6,5,4,3,2,1,0:T(8,128)(2,1)}, bf16[8,2,2,16,128]{4,3,2,1,0:T(8,128)(2,1)}, bf16[8,2,2,16,128]{4,3,2,1,0:T(8,128)(2,1)}) custom-call(s32[128]{0:T(128)} %get-tuple-element.22.vehicle_ref, s32[128]{0:T(128)} %get-tuple-element.21.tile_ref, bf16[8,8,2,2,16,128]{5,4,3,2,1,0:T(8,128)(2,1)} %bitcast.11), custom_call_target="tpu_custom_call" | custom-call | tf_op jit(solution)/shard_map/exchange/pallas_call | solution.py:351
  112.6 20.4 %agent_stage.1.joined_ref = bf16[8,8,64,128]{3,2,1,0:T(8,128)(2,1)} custom-call(s32[64]{0:T(128)} %reshape.271.slot_ref, s32[64]{0:T(128)} %reshape.272.live_ref, bf16[8,8,64,128]{3,2,1,0:T(8,128)(2,1)} %bev_ref.1, bf16[128,8,32,128]{3,2,1,0:T(8,128)(2,1)} %bitcast.7, bf16[128,8,32,128]{3,2,1,0:T(8,128)(2,1)} %bitcast.8, bf16[128,8,32,128]{3,2,1,0:T(8,128)(2,1)} %bitcast.9, ...), custom_call_target="tpu_custom_call" | custom-call | tf_op jit(solution)/shard_map/agent_stage/pallas_call | solution.py:88
  133.1 1.0 fusion.24
  134.0 1.3 collective-permute-start.1
  135.3 4.0 %collective-permute-start = (bf16[8,1,64,128]{3,2,1,0:T(8,128)(2,1)S(1)}, bf16[8,1,64,128]{3,2,1,0:T(8,128)(2,1)S(1)}, u32[]{:S(2)}, u32[]{:S(2)}) collective-permute-start(bf16[8,1,64,128]{3,2,1,0:T(8,128)(2,1)S(1)} %get-tuple-element.16), channel_id=1, source_target_pairs={{0,1},{1,2},{2,3},{4,5},{5,6},{6,7},{8,9},{9,10},{10,11},{12,13},{... | collective-permute-start | bytes 393224 | tf_op jit(solution)/shard_map/ppermute | solution.py:378
  139.3 1.7 collective-permute-done.1.joined_down
  141.0 0.9 collective-permute-done.joined_up
  141.9 0.6 copy-done.1
  142.5 29.2 %layer_stage.1 = bf16[8,8,64,256]{3,2,1,0:T(8,128)(2,1)} custom-call(bf16[8,8,64,128]{3,2,1,0:T(8,128)(2,1)} %bev_ref.1, bf16[8,8,64,128]{3,2,1,0:T(8,128)(2,1)} %agent_stage.1.joined_ref, bf16[8,1,64,128]{3,2,1,0:T(8,128)(2,1)} %bitcast.12, bf16[8,1,64,128]{3,2,1,0:T(8,128)(2,1)} %bitcast.13, bf16[8,1,64,128]{3,2,1,0:T(8,128)(2,1)} %copy-done.1, ...), custom_call_target="tpu_custom_call" | custom-call | tf_op jit(solution)/shard_map/layer_stage/pallas_call | solution.py:213
  (26 shorter events, 0.8 us)
Async XLA Ops:
  134.0 7.0 %collective-permute-start.1 = (bf16[8,1,64,128]{3,2,1,0:T(8,128)(2,1)S(1)}, bf16[8,1,64,128]{3,2,1,0:T(8,128)(2,1)S(1)}, u32[]{:S(2)}, u32[]{:S(2)}) collective-permute-start(bf16[8,1,64,128]{3,2,1,0:T(8,128)(2,1)S(1)} %get-tuple-element.15), channel_id=1, source_target_pairs={{1,0},{2,1},{3,2},{5,4},{6,5},{7,6},{9,8},{10,9},{11,10},{13,12},{... | collective-permute-start | bytes 393224 | tf_op jit(solution)/shard_map/ppermute | solution.py:379
  135.3 6.6 %collective-permute-start = (bf16[8,1,64,128]{3,2,1,0:T(8,128)(2,1)S(1)}, bf16[8,1,64,128]{3,2,1,0:T(8,128)(2,1)S(1)}, u32[]{:S(2)}, u32[]{:S(2)}) collective-permute-start(bf16[8,1,64,128]{3,2,1,0:T(8,128)(2,1)S(1)} %get-tuple-element.16), channel_id=1, source_target_pairs={{0,1},{1,2},{2,3},{4,5},{5,6},{6,7},{8,9},{9,10},{10,11},{12,13},{... | collective-permute-start | bytes 393224 | tf_op jit(solution)/shard_map/ppermute | solution.py:378
  141.0 0.9 copy-start
  141.9 0.6 copy-start.1

commit v4 on v3

--- a/solution.py
+++ b/solution.py
@@ -28,39 +28,6 @@
     return jnp.dot(jnp.concatenate(halves(x), axis=-1), member, preferred_element_type=f32)
 
 
-def agent_kernel(slot_ref, live_ref, ego_ref, t0, t1, t2, t3, query_ref, keyvalue_ref, out_w_ref,
-                 scale_ref, joined_ref):
-    step = pl.program_id(0)
-    tiles = (t0, t1, t2, t3)
-    height, cols, channels = ego_ref.shape[1:]
-    cells = height * cols
-    ego = ego_ref[0].reshape(cells, channels)
-    member = member_matrix(channels)
-    query = jnp.dot(ego, query_ref[...], preferred_element_type=f32)
-    count = len(tiles) + 1
-    sources = jnp.concatenate([ego] + [t[0].reshape(cells, channels) for t in tiles], axis=0)
-    keyvalue = jnp.dot(sources, keyvalue_ref[...], preferred_element_type=f32).astype(bf16)
-    query = query * (lax.rsqrt(head_sums(query * query, member) + unit_eps) * scale_row(scale_ref, 0, channels))
-    key = keyvalue[:, :channels].astype(f32)
-    norms = head_sums(key * key, member)
-    products = head_sums((key.reshape(count, cells, channels) * query[None]).reshape(count * cells, channels), member)
-    score = products * lax.rsqrt(norms + unit_eps)
-    scores = [score[a * cells : (a + 1) * cells] for a in range(count)]
-    values = [keyvalue[a * cells : (a + 1) * cells, channels:] for a in range(count)]
-    for a in range(len(tiles)):
-        scores[a + 1] = scores[a + 1] + jnp.where(live_ref[step * len(tiles) + a] > 0, 0.0, -1e30)
-    top = functools.reduce(jnp.maximum, scores)
-    total, mix = None, None
-    for score, value in zip(scores, values):
-        weight = jnp.exp(score - top)
-        total = weight if total is None else total + weight
-        part = weight * value.astype(f32)
-        mix = part if mix is None else mix + part
-    mix = (mix / total).astype(bf16)
-    joined = jnp.dot(mix, out_w_ref[...], preferred_element_type=f32).astype(bf16)
-    joined_ref[0] = joined.reshape(height, cols, channels)
-
-
 def member_matrix(width):
     rows = lax.broadcasted_iota(jnp.int32, (2 * width, width), 0) % width // HEAD
     lanes = lax.broadcasted_iota(jnp.int32, (2 * width, width), 1) // HEAD
@@ -73,33 +40,6 @@
     for j in range(1, width // HEAD):
         row = jnp.where(head == j, scale_ref[first + j], row)
     return row
-
-
-def agent_stage(bev_maps, arrived, slots, live, agent_query, agent_keyvalue, agent_out, agent_scale):
-    vehicles, height, width_cells, channels = bev_maps.shape
-    tile_cols = width_cells // TILE
-    agents = slots.shape[1]
-    full = lambda i, *_: (0, 0)
-    ego_spec = pl.BlockSpec((1, height, TILE, channels), lambda i, *_: (i // tile_cols, 0, i % tile_cols, 0))
-    tile_specs = [
-        pl.BlockSpec((1, height, TILE, channels), lambda i, s, l, a=a: (s[i * agents + a], 0, 0, 0))
-        for a in range(agents)
-    ]
-    return pl.pallas_call(
-        agent_kernel,
-        grid_spec=pltpu.PrefetchScalarGridSpec(
-            num_scalar_prefetch=2,
-            grid=(vehicles * tile_cols,),
-            in_specs=[ego_spec, *tile_specs]
-            + [pl.BlockSpec(w.shape, full) for w in (agent_query, agent_keyvalue, agent_out)]
-            + [pl.BlockSpec(memory_space=pltpu.SMEM)],
-            out_specs=ego_spec,
-        ),
-        out_shape=jax.ShapeDtypeStruct(bev_maps.shape, bf16),
-        compiler_params=pltpu.CompilerParams(dimension_semantics=("arbitrary",)),
-        name="agent_stage",
-    )(slots.reshape(-1), live.reshape(-1), bev_maps, arrived, arrived, arrived, arrived, agent_query,
-      agent_keyvalue, agent_out, agent_scale)
 
 
 def layer_norm(x, gain):
@@ -227,14 +167,18 @@
 PLANE = 8
 HOPS = (0, -1, 1, -2, 2, -3, 3, 4)
 PIECES = 2
+SHARES = 2
 SLOTS = 2
 
 
-def exchange_kernel(vehicle_ref, tile_ref, maps_ref, arrived_ref, up_ref, down_ref, *scratch):
-    outbox, ring_send, ring_recv, plane_send, plane_recv, own_sem, edge_send, edge_recv = scratch[-8:]
+def join_kernel(vehicle_ref, tile_ref, slot_ref, bias_ref, scale_ref, maps_ref, query_ref, keyvalue_ref,
+                out_w_ref, joined_ref, bev_up, bev_down, joined_up, joined_down, *scratch):
+    (ring_send, ring_recv, plane_send, plane_recv, edge_send, edge_recv, outbox) = scratch[-7:]
+    inboxes = scratch[-7 - PIECES : -7]
     me = lax.axis_index("veh")
     plane, seat = me // PLANE, me % PLANE
-    height = maps_ref.shape[1]
+    vehicles, height, tile_cols, _, part, channels = maps_ref.shape
+    depth = vehicles // SHARES
     bands = lax.axis_size("row")
     band = lax.axis_index("row")
     below = {"row": lax.rem(band + 1, bands)}
@@ -250,134 +194,191 @@
 
     started = []
 
-    def held(block, piece):
-        if block == 0:
-            return maps_ref.at[:, :, :, piece]
-        return scratch[(block - 1) * PIECES + piece]
-
-    def pass_on(source, block, piece, target):
+    def send(src, dst, send_sem, recv_sem, target):
         copy = pltpu.make_async_remote_copy(
-            src_ref=held(source, piece),
-            dst_ref=held(block, piece),
-            send_sem=ring_send.at[block - 1, piece],
-            recv_sem=ring_recv.at[block - 1, piece],
+            src_ref=src,
+            dst_ref=dst,
+            send_sem=send_sem,
+            recv_sem=recv_sem,
             device_id=target,
             device_id_type=pl.DeviceIdType.MESH,
         )
         copy.start()
-        started.append(copy)
-
-    def arrival(block, piece):
-        ref = held(block, piece)
-        pltpu.make_async_copy(ref, ref, ring_recv.at[block - 1, piece]).wait()
+        return copy
+
+    def settle(ref, sem):
+        pltpu.make_async_copy(ref, ref, sem).wait()
+
+    def held(block, piece, share=None):
+        span = slice(None) if share is None else pl.ds(share * depth, depth)
+        if block == 0:
+            return maps_ref.at[span, :, :, piece]
+        return scratch[(block - 1) * PIECES + piece].at[span]
+
+    def pass_on(source, block, piece, share, target):
+        sems = (ring_send.at[block - 1, piece, share], ring_recv.at[block - 1, piece, share])
+        started.append(send(held(source, piece, share), held(block, piece, share), *sems, target))
+
+    def relay(block, piece):
+        front = block % 2 == 1
+        for share in range(SHARES):
+            settle(held(block, piece, share), ring_recv.at[block - 1, piece, share])
+            if block < RING - 3:
+                pass_on(block, block + 2, piece, share, ahead if front else behind)
+            elif block < RING - 1 and front == (piece < PIECES // 2):
+                pass_on(block, RING - 1, piece, share, ahead if front else behind)
 
     def hand_out(block, piece):
-        source = held(block, piece)
+        source = maps_ref if block == 0 else scratch[(block - 1) * PIECES + piece]
+
+        def pick(j, slot):
+            at = (block * PLANE + j) * SLOTS + slot
+            if block == 0:
+                return source[vehicle_ref[at], :, tile_ref[at], piece]
+            return source[vehicle_ref[at], :, tile_ref[at]]
 
         def fill(j, carry):
             for slot in range(SLOTS):
-                at = (block * PLANE + j) * SLOTS + slot
-                outbox[block, j, slot, :, piece] = source[vehicle_ref[at], :, tile_ref[at]]
+                outbox[piece, block, j, slot] = pick(j, slot)
             return carry
 
-        lax.fori_loop(0, PLANE, fill, 0)
+        lax.fori_loop(1, PLANE, fill, 0)
+        place = (block * PLANE + seat) * SLOTS
         for j in range(1, PLANE):
-            pltpu.make_async_remote_copy(
-                src_ref=outbox.at[block, j, :, :, piece],
-                dst_ref=arrived_ref.at[block, seat, :, :, piece],
-                send_sem=plane_send.at[0],
-                recv_sem=plane_recv.at[0],
-                device_id=peers[j],
-                device_id_type=pl.DeviceIdType.MESH,
-            ).start()
-
-    edges = []
-    for at, (row, ref, target) in enumerate(((height - 1, up_ref, below), (0, down_ref, above))):
-        edge = pltpu.make_async_remote_copy(
-            src_ref=maps_ref.at[:, row],
-            dst_ref=ref,
-            send_sem=edge_send.at[at],
-            recv_sem=edge_recv.at[at],
-            device_id=target,
-            device_id_type=pl.DeviceIdType.MESH,
-        )
-        edge.start()
-        edges.append(edge)
+            send(outbox.at[piece, block, j], inboxes[piece].at[pl.ds(place, SLOTS)], plane_send.at[piece],
+                 plane_recv.at[piece], peers[j])
+        for slot in range(SLOTS):
+            inboxes[piece][place + slot] = pick(0, slot)
+
+    def attend(piece, vehicle):
+        flat = lambda x: x.reshape(height * part, channels)
+        agents = bias_ref.shape[0] // (vehicles * tile_cols)
+        count = agents + 1
+        half = height * part
+        cells = half * tile_cols
+        member = member_matrix(channels)
+        ego = jnp.concatenate([flat(maps_ref[vehicle, :, t, piece]) for t in range(tile_cols)], axis=0)
+        row = lambda t, a: (vehicle * tile_cols + t) * agents + a
+        sent = [
+            flat(inboxes[piece][slot_ref[row(t, a)]]) for a in range(agents) for t in range(tile_cols)
+        ]
+        sources = jnp.concatenate([ego] + sent, axis=0)
+        query = jnp.dot(ego, query_ref[...], preferred_element_type=f32)
+        keyvalue = jnp.dot(sources, keyvalue_ref[...], preferred_element_type=f32).astype(bf16)
+        norm = lax.rsqrt(head_sums(query * query, member) + unit_eps)
+        query = query * (norm * scale_row(scale_ref, 0, channels))
+        key = keyvalue[:, :channels].astype(f32)
+        norms = head_sums(key * key, member)
+        products = key.reshape(count, cells, channels) * query[None]
+        products = head_sums(products.reshape(count * cells, channels), member)
+        score = products * lax.rsqrt(norms + unit_eps)
+        scores = [score[:cells]]
+        for a in range(agents):
+            tops = [cells * (a + 1) + half * t for t in range(tile_cols)]
+            biased = [score[at : at + half] + bias_ref[row(t, a)] for t, at in enumerate(tops)]
+            scores.append(jnp.concatenate(biased, axis=0))
+        top = functools.reduce(jnp.maximum, scores)
+        total, mix = None, None
+        for a, one in enumerate(scores):
+            weight = jnp.exp(one - top)
+            total = weight if total is None else total + weight
+            value = weight * keyvalue[a * cells : (a + 1) * cells, channels:].astype(f32)
+            mix = value if mix is None else mix + value
+        mix = (mix / total).astype(bf16)
+        joined = jnp.dot(mix, out_w_ref[...], preferred_element_type=f32).astype(bf16)
+        for t in range(tile_cols):
+            joined_ref[vehicle, :, t, piece] = joined[t * half : (t + 1) * half].reshape(
+                height, part, channels
+            )
+
+    def attend_span(piece, first, last):
+        def one(vehicle, carry):
+            attend(piece, vehicle)
+            return carry
+
+        lax.fori_loop(first, last, one, 0)
+
+    def send_edges(piece):
+        for at, (row, ref, target) in enumerate(((height - 1, joined_up, below), (0, joined_down, above))):
+            src = joined_ref.at[:, row, :, piece]
+            sems = (edge_send.at[1 + piece, at], edge_recv.at[1 + piece, at])
+            edges.append(send(src, ref.at[:, :, piece], *sems, target))
+
+    edges = [
+        send(maps_ref.at[:, height - 1], bev_up, edge_send.at[0, 0], edge_recv.at[0, 0], below),
+        send(maps_ref.at[:, 0], bev_down, edge_send.at[0, 1], edge_recv.at[0, 1], above),
+    ]
+    far = RING - 1
+    for share in range(SHARES):
+        pass_on(0, 1, 0, share, ahead)
+        pass_on(0, 2, 0, share, behind)
+    hand_out(0, 0)
+    hand_out(0, 1)
+    for block in (1, 2, 3, 4):
+        relay(block, 0)
+        hand_out(block, 0)
+    for share in range(SHARES):
+        pass_on(0, 2, 1, share, behind)
+    relay(5, 0)
+    for share in range(SHARES):
+        pass_on(0, 1, 1, share, ahead)
+    relay(6, 0)
+    hand_out(5, 0)
+    hand_out(6, 0)
+    relay(far, 0)
+    hand_out(far, 0)
+    for block in (2, 4, 1):
+        relay(block, 1)
+        hand_out(block, 1)
+    settle(inboxes[0].at[pl.ds(0, (PLANE - 1) * RING * SLOTS)], plane_recv.at[0])
+    attend_span(0, 0, vehicles // 2)
+    for block in (6, 3):
+        relay(block, 1)
+        hand_out(block, 1)
+    attend_span(0, vehicles // 2, vehicles)
+    send_edges(0)
+    for block in (far, 5):
+        relay(block, 1)
+        hand_out(block, 1)
+    settle(inboxes[1].at[pl.ds(0, (PLANE - 1) * RING * SLOTS)], plane_recv.at[1])
+    attend_span(1, 0, vehicles)
+    send_edges(1)
+    for copy in started:
+        copy.wait_send()
     for piece in range(PIECES):
-        pass_on(0, 1, piece, ahead)
-        pass_on(0, 2, piece, behind)
-    for piece in range(PIECES):
-        hand_out(0, piece)
-    for step in range(1, RING // 2):
-        front, back = 2 * step - 1, 2 * step
-        for piece in range(PIECES):
-            arrival(front, piece)
-            if step < RING // 2 - 1:
-                pass_on(front, front + 2, piece, ahead)
-            elif piece < PIECES // 2:
-                pass_on(front, RING - 1, piece, ahead)
-            arrival(back, piece)
-            if step < RING // 2 - 1:
-                pass_on(back, back + 2, piece, behind)
-            elif piece >= PIECES // 2:
-                pass_on(back, RING - 1, piece, behind)
-            hand_out(front, piece)
-            hand_out(back, piece)
-    for piece in range(PIECES):
-        arrival(RING - 1, piece)
-        hand_out(RING - 1, piece)
-    for block in range(RING):
-        pltpu.make_async_copy(outbox.at[block, 0], arrived_ref.at[block, seat], own_sem.at[block]).start()
+        settle(outbox.at[piece, pl.ds(0, PLANE - 1)], plane_send.at[piece])
     for edge in edges:
         edge.wait()
-    for copy in started:
-        copy.wait_send()
-    sent = outbox.at[pl.ds(0, PLANE - 1)]
-    pltpu.make_async_copy(sent, sent, plane_send.at[0]).wait()
-    got = arrived_ref.at[pl.ds(0, PLANE - 1)]
-    pltpu.make_async_copy(got, got, plane_recv.at[0]).wait()
-    for block in range(RING):
-        pltpu.make_async_copy(outbox.at[block, 0], arrived_ref.at[block, seat], own_sem.at[block]).wait()
-
-
-def exchange(bev_maps, picks):
+
+
+def join_stage(bev_maps, picks, slots, bias, agent_query, agent_keyvalue, agent_out, agent_scale):
     vehicles, height, width_cells, channels = bev_maps.shape
     tile_cols = width_cells // TILE
     part = TILE // PIECES
     tiled = bev_maps.reshape(vehicles, height, tile_cols, PIECES, part, channels)
-    box = (RING, PLANE, SLOTS, height, PIECES, part, channels)
     edge = (vehicles,) + tiled.shape[2:]
-    shapes = (box, edge, edge)
-    arrived, up, down = pl.pallas_call(
-        exchange_kernel,
-        in_specs=[pl.BlockSpec(memory_space=pltpu.SMEM)] * 2 + [pl.BlockSpec(memory_space=pltpu.VMEM)],
-        out_specs=[pl.BlockSpec(memory_space=pl.ANY)] * 3,
-        out_shape=[jax.ShapeDtypeStruct(s, bf16) for s in shapes],
-        scratch_shapes=[pltpu.VMEM(tiled.shape[:3] + tiled.shape[4:], bf16)] * ((RING - 1) * PIECES)
-        + [
-            pltpu.VMEM(box, bf16),
-            pltpu.SemaphoreType.DMA((RING - 1, PIECES)),
-            pltpu.SemaphoreType.DMA((RING - 1, PIECES)),
-            pltpu.SemaphoreType.DMA((1,)),
-            pltpu.SemaphoreType.DMA((1,)),
-            pltpu.SemaphoreType.DMA((RING,)),
-            pltpu.SemaphoreType.DMA((2,)),
-            pltpu.SemaphoreType.DMA((2,)),
-        ],
+    block = tiled.shape[:3] + tiled.shape[4:]
+    scalars = pl.BlockSpec(memory_space=pltpu.SMEM)
+    vectors = pl.BlockSpec(memory_space=pltpu.VMEM)
+    ring = pltpu.SemaphoreType.DMA((RING - 1, PIECES, SHARES))
+    per_piece = pltpu.SemaphoreType.DMA((PIECES,))
+    per_edge = pltpu.SemaphoreType.DMA((1 + PIECES, 2))
+    outs = pl.pallas_call(
+        join_kernel,
+        in_specs=[scalars] * 5 + [vectors] * 4,
+        out_specs=[vectors] + [pl.BlockSpec(memory_space=pl.ANY)] * 4,
+        out_shape=[jax.ShapeDtypeStruct(tiled.shape, bf16)] + [jax.ShapeDtypeStruct(edge, bf16)] * 4,
+        scratch_shapes=[pltpu.VMEM(block, bf16)] * ((RING - 1) * PIECES)
+        + [pltpu.VMEM((RING * PLANE * SLOTS, height, part, channels), bf16)] * PIECES
+        + [ring, ring, per_piece, per_piece, per_edge, per_edge]
+        + [pltpu.VMEM((PIECES, RING, PLANE, SLOTS, height, part, channels), bf16)],
         compiler_params=pltpu.CompilerParams(collective_id=0, has_side_effects=True),
-        name="exchange",
-    )(picks // tile_cols, picks % tile_cols, tiled)
+        name="join_stage",
+    )(picks // tile_cols, picks % tile_cols, slots.reshape(-1), bias.reshape(-1), agent_scale, tiled,
+      agent_query, agent_keyvalue, agent_out)
     flat = (vehicles, 1, width_cells, channels)
-    return arrived.reshape(-1, height, TILE, channels), (up.reshape(flat), down.reshape(flat))
-
-
-def row_halo(cells):
-    count = lax.axis_size("row")
-    height = cells.shape[1]
-    return (
-        lax.ppermute(cells[:, height - 1 :], "row", [(i, i + 1) for i in range(count - 1)]),
-        lax.ppermute(cells[:, :1], "row", [(i + 1, i) for i in range(count - 1)]),
-    )
+    edges = [x.reshape(flat) for x in outs[1:]]
+    return outs[0].reshape(bev_maps.shape), edges[:2], edges[2:]
 
 
 def route(senders, shifts, counts, vehicles_here, tile_cols):
@@ -422,18 +423,16 @@
     slots = slots - jnp.maximum(-my_shift, 0)[:, None]
     slots = jnp.where(inside, slots, 0)
     per_tile = lambda x: x.reshape(vehicles_here, agents, tile_cols).transpose(0, 2, 1).reshape(-1, agents)
-    return picks, per_tile(slots), per_tile(inside.astype(jnp.int32))
+    return picks, per_tile(slots), per_tile(jnp.where(inside, 0.0, -1e30))
 
 
 def on_device(bev_maps, senders, shifts, counts, agent_query, agent_keyvalue, agent_out, agent_scale,
               conv_weight, gain_first, window_in, window_out, window_scale, gain_second, hidden_up,
               hidden_down):
     vehicles_here, height, width_cells, channels = bev_maps.shape
-    picks, slots, live = route(senders, shifts, counts, vehicles_here, width_cells // TILE)
-    arrived, bev_halo = exchange(bev_maps, picks)
-    joined = agent_stage(bev_maps, arrived, slots, live, agent_query, agent_keyvalue, agent_out,
-                         agent_scale)
-    joined_halo = row_halo(joined)
+    picks, slots, bias = route(senders, shifts, counts, vehicles_here, width_cells // TILE)
+    joined, bev_halo, joined_halo = join_stage(bev_maps, picks, slots, bias, agent_query,
+                                               agent_keyvalue, agent_out, agent_scale)
     return layer_stage(bev_maps, joined, bev_halo, joined_halo, conv_weight, gain_first, window_in,
                        window_out, window_scale, gain_second, hidden_up, hidden_down)
 

time: 173 us -> 156 us (0.902)
  Pallas kernels: 155 us -> 148 us
  starting transfers between devices: 5.29 us -> 0 us
  waiting for transfers between devices: 2.55 us -> 0 us
    pallas_call x2 -> x1, Pallas kernels: 125 us -> 119 us  [join_stage(): pl.pallas_call(join_kernel, in_specs=[scalars] * 5 + [vectors] * 4, out_s...]
    ppermute x2 -> x0, starting transfers between devices: 5.29 us -> none  [the longest x1 3.99 us: row_halo(): lax.ppermute(cells[:, height - 1:], 'row', [(i, i + 1) for i in range(cou...]
    ppermute x2 -> x0, waiting for transfers between devices: 2.55 us -> none  [the longest x1 1.65 us: row_halo(): lax.ppermute(cells[:, :1], 'row', [(i + 1, i) for i in range(count - 1)])]
  transfers between devices with their start and end apart: 2 -> 0, of which waited for: 2 -> 0; matrix products, arithmetic and copies ran while one was open for 0% -> 0% of each run, Pallas kernels for 0% -> 0%
where the time goes in v4:
time: 156 us
  Pallas kernels  148 us (95%)
  local copies, waits for them, and re-layouts  4.92 us (3%)
  other arithmetic  2.53 us (2%)
    pallas_call x1, Pallas kernels, join_stage(): pl.pallas_call(join_kernel, in_specs=[scalars] * 5 + [vectors] * 4, out_s...  119 us
    pallas_call x1, Pallas kernels, layer_stage(): pl.pallas_call(layer_kernel, grid=(vehicles,), in_specs=[block, block, ed...  29.3 us

profile of v4, /device:TPU:1, one launch (start us, length us, event | category | flops | bytes accessed | tf_op | source)
XLA Modules:
  0.0 155.7 jit_solution(11120408329927086958)
XLA Ops:
  0.0 0.7 and_select_fusion.3
  0.7 0.1 fusion.11
  0.8 0.1 lt.102
  0.8 0.8 reshape.269
  1.6 0.1 copy.23
  1.8 0.8 copy.22
  2.6 0.1 reshape.268
  2.8 0.1 squeeze.10
  2.9 0.1 broadcast_compare_fusion
  3.0 0.8 copy.25
  3.8 0.1 reshape.270
  4.0 0.3 select_reduce_fusion
  4.3 0.1 and.157
  4.4 0.1 squeeze.11
  4.5 0.1 add.192
  4.7 0.7 reshape.279.slot_ref
  5.4 0.6 reshape.282.bias_ref
  6.0 0.4 select_reduce_fusion.1
  6.4 0.4 multiply_reduce_fusion
  6.7 0.1 copy.26
  6.9 0.1 reshape.271
  7.0 0.6 and_select_fusion
  7.6 118.8 %join_stage.1 = (bf16[8,8,2,2,16,128]{5,4,3,2,1,0:T(8,128)(2,1)}, bf16[8,2,2,16,128]{4,3,2,1,0:T(8,128)(2,1)}, bf16[8,2,2,16,128]{4,3,2,1,0:T(8,128)(2,1)}, bf16...) custom-call(s32[128]{0:T(128)} %get-tuple-element.23.vehicle_ref, s32[128]{0:T(128)} %get-tuple-element.22.tile_ref, ...), custom_call_target="tpu_custom_call" | custom-call | tf_op jit(solution)/shard_map/join_stage/pallas_call | solution.py:366
  126.4 29.3 %layer_stage.1 = bf16[8,8,64,256]{3,2,1,0:T(8,128)(2,1)} custom-call(bf16[8,8,64,128]{3,2,1,0:T(8,128)(2,1)} %bev_ref.1, bf16[8,8,64,128]{3,2,1,0:T(8,128)(2,1)} %bitcast.10, bf16[8,1,64,128]{3,2,1,0:T(8,128)(2,1)} %bitcast.11, bf16[8,1,64,128]{3,2,1,0:T(8,128)(2,1)} %bitcast.12, bf16[8,1,64,128]{3,2,1,0:T(8,128)(2,1)} %bitcast.13, ...), custom_call_target="tpu_custom_call" | custom-call | tf_op jit(solution)/shard_map/layer_stage/pallas_call | solution.py:153
  (16 shorter events, 0.3 us)

commit v5 on v4

--- a/solution.py
+++ b/solution.py
@@ -173,8 +173,9 @@
 
 def join_kernel(vehicle_ref, tile_ref, slot_ref, bias_ref, scale_ref, maps_ref, query_ref, keyvalue_ref,
                 out_w_ref, joined_ref, bev_up, bev_down, joined_up, joined_down, *scratch):
-    (ring_send, ring_recv, plane_send, plane_recv, edge_send, edge_recv, outbox) = scratch[-7:]
-    inboxes = scratch[-7 - PIECES : -7]
+    (ring_send, ring_recv, plane_send, plane_recv, edge_send, edge_recv, outbox, ego_query, ego_keyvalue,
+     ego_score) = scratch[-10:]
+    inboxes = scratch[-10 - PIECES : -10]
     me = lax.axis_index("veh")
     plane, seat = me // PLANE, me % PLANE
     vehicles, height, tile_cols, _, part, channels = maps_ref.shape
@@ -250,39 +251,49 @@
         for slot in range(SLOTS):
             inboxes[piece][place + slot] = pick(0, slot)
 
-    def attend(piece, vehicle):
-        flat = lambda x: x.reshape(height * part, channels)
-        agents = bias_ref.shape[0] // (vehicles * tile_cols)
-        count = agents + 1
-        half = height * part
-        cells = half * tile_cols
+    half = height * part
+    cells = half * tile_cols
+    flat = lambda x: x.reshape(half, channels)
+
+    def prepare(piece, vehicle):
         member = member_matrix(channels)
         ego = jnp.concatenate([flat(maps_ref[vehicle, :, t, piece]) for t in range(tile_cols)], axis=0)
+        query = jnp.dot(ego, query_ref[...], preferred_element_type=f32)
+        keyvalue = jnp.dot(ego, keyvalue_ref[...], preferred_element_type=f32).astype(bf16)
+        norm = lax.rsqrt(head_sums(query * query, member) + unit_eps)
+        query = query * (norm * scale_row(scale_ref, 0, channels))
+        key = keyvalue[:, :channels].astype(f32)
+        norm = lax.rsqrt(head_sums(key * key, member) + unit_eps)
+        ego_query[vehicle] = query
+        ego_keyvalue[vehicle] = keyvalue[:, channels:]
+        ego_score[vehicle] = head_sums(query * key, member) * norm
+
+    def attend(piece, vehicle):
+        agents = bias_ref.shape[0] // (vehicles * tile_cols)
+        member = member_matrix(channels)
         row = lambda t, a: (vehicle * tile_cols + t) * agents + a
         sent = [
             flat(inboxes[piece][slot_ref[row(t, a)]]) for a in range(agents) for t in range(tile_cols)
         ]
-        sources = jnp.concatenate([ego] + sent, axis=0)
-        query = jnp.dot(ego, query_ref[...], preferred_element_type=f32)
+        sources = jnp.concatenate(sent, axis=0)
         keyvalue = jnp.dot(sources, keyvalue_ref[...], preferred_element_type=f32).astype(bf16)
-        norm = lax.rsqrt(head_sums(query * query, member) + unit_eps)
-        query = query * (norm * scale_row(scale_ref, 0, channels))
         key = keyvalue[:, :channels].astype(f32)
         norms = head_sums(key * key, member)
-        products = key.reshape(count, cells, channels) * query[None]
-        products = head_sums(products.reshape(count * cells, channels), member)
+        products = key.reshape(agents, cells, channels) * ego_query[vehicle][None]
+        products = head_sums(products.reshape(agents * cells, channels), member)
         score = products * lax.rsqrt(norms + unit_eps)
-        scores = [score[:cells]]
+        scores, values = [ego_score[vehicle]], [ego_keyvalue[vehicle]]
         for a in range(agents):
-            tops = [cells * (a + 1) + half * t for t in range(tile_cols)]
+            tops = [cells * a + half * t for t in range(tile_cols)]
             biased = [score[at : at + half] + bias_ref[row(t, a)] for t, at in enumerate(tops)]
             scores.append(jnp.concatenate(biased, axis=0))
+            values.append(keyvalue[a * cells : (a + 1) * cells, channels:])
         top = functools.reduce(jnp.maximum, scores)
         total, mix = None, None
         for a, one in enumerate(scores):
             weight = jnp.exp(one - top)
             total = weight if total is None else total + weight
-            value = weight * keyvalue[a * cells : (a + 1) * cells, channels:].astype(f32)
+            value = weight * values[a].astype(f32)
             mix = value if mix is None else mix + value
         mix = (mix / total).astype(bf16)
         joined = jnp.dot(mix, out_w_ref[...], preferred_element_type=f32).astype(bf16)
@@ -291,22 +302,22 @@
                 height, part, channels
             )
 
-    def attend_span(piece, first, last):
+    def over(task, piece, first, last):
         def one(vehicle, carry):
-            attend(piece, vehicle)
+            task(piece, vehicle)
             return carry
 
         lax.fori_loop(first, last, one, 0)
 
-    def send_edges(piece):
+    def send_edges(piece, share):
+        span = pl.ds(share * depth, depth)
         for at, (row, ref, target) in enumerate(((height - 1, joined_up, below), (0, joined_down, above))):
-            src = joined_ref.at[:, row, :, piece]
-            sems = (edge_send.at[1 + piece, at], edge_recv.at[1 + piece, at])
-            edges.append(send(src, ref.at[:, :, piece], *sems, target))
+            sems = (edge_send.at[1 + piece, share, at], edge_recv.at[1 + piece, share, at])
+            edges.append(send(joined_ref.at[span, row, :, piece], ref.at[span, :, piece], *sems, target))
 
     edges = [
-        send(maps_ref.at[:, height - 1], bev_up, edge_send.at[0, 0], edge_recv.at[0, 0], below),
-        send(maps_ref.at[:, 0], bev_down, edge_send.at[0, 1], edge_recv.at[0, 1], above),
+        send(maps_ref.at[:, height - 1], bev_up, edge_send.at[0, 0, 0], edge_recv.at[0, 0, 0], below),
+        send(maps_ref.at[:, 0], bev_down, edge_send.at[0, 0, 1], edge_recv.at[0, 0, 1], above),
     ]
     far = RING - 1
     for share in range(SHARES):
@@ -317,6 +328,8 @@
     for block in (1, 2, 3, 4):
         relay(block, 0)
         hand_out(block, 0)
+        if block in (2, 4):
+            over(prepare, 0, (block - 2) // 2 * depth, block // 2 * depth)
     for share in range(SHARES):
         pass_on(0, 2, 1, share, behind)
     relay(5, 0)
@@ -331,18 +344,21 @@
         relay(block, 1)
         hand_out(block, 1)
     settle(inboxes[0].at[pl.ds(0, (PLANE - 1) * RING * SLOTS)], plane_recv.at[0])
-    attend_span(0, 0, vehicles // 2)
+    over(attend, 0, 0, depth)
     for block in (6, 3):
         relay(block, 1)
         hand_out(block, 1)
-    attend_span(0, vehicles // 2, vehicles)
-    send_edges(0)
+    over(attend, 0, depth, vehicles)
+    for share in range(SHARES):
+        send_edges(0, share)
     for block in (far, 5):
         relay(block, 1)
         hand_out(block, 1)
+    over(prepare, 1, 0, vehicles)
     settle(inboxes[1].at[pl.ds(0, (PLANE - 1) * RING * SLOTS)], plane_recv.at[1])
-    attend_span(1, 0, vehicles)
-    send_edges(1)
+    for share in range(SHARES):
+        over(attend, 1, share * depth, (share + 1) * depth)
+        send_edges(1, share)
     for copy in started:
         copy.wait_send()
     for piece in range(PIECES):
@@ -362,7 +378,7 @@
     vectors = pl.BlockSpec(memory_space=pltpu.VMEM)
     ring = pltpu.SemaphoreType.DMA((RING - 1, PIECES, SHARES))
     per_piece = pltpu.SemaphoreType.DMA((PIECES,))
-    per_edge = pltpu.SemaphoreType.DMA((1 + PIECES, 2))
+    per_edge = pltpu.SemaphoreType.DMA((1 + PIECES, SHARES, 2))
     outs = pl.pallas_call(
         join_kernel,
         in_specs=[scalars] * 5 + [vectors] * 4,
@@ -371,7 +387,8 @@
         scratch_shapes=[pltpu.VMEM(block, bf16)] * ((RING - 1) * PIECES)
         + [pltpu.VMEM((RING * PLANE * SLOTS, height, part, channels), bf16)] * PIECES
         + [ring, ring, per_piece, per_piece, per_edge, per_edge]
-        + [pltpu.VMEM((PIECES, RING, PLANE, SLOTS, height, part, channels), bf16)],
+        + [pltpu.VMEM((PIECES, RING, PLANE, SLOTS, height, part, channels), bf16)]
+        + [pltpu.VMEM((vehicles, height * part * tile_cols, channels), t) for t in (f32, bf16, f32)],
         compiler_params=pltpu.CompilerParams(collective_id=0, has_side_effects=True),
         name="join_stage",
     )(picks // tile_cols, picks % tile_cols, slots.reshape(-1), bias.reshape(-1), agent_scale, tiled,
@@ -383,11 +400,11 @@
 
 def route(senders, shifts, counts, vehicles_here, tile_cols):
     agents = senders.shape[1]
-    devices = lax.axis_size("veh")
     myself = lax.axis_index("veh")
     plane, seat = myself // PLANE, myself % PLANE
     pair_count = vehicles_here * agents
-    by_block = lambda x: lax.dynamic_slice_in_dim(x.reshape(devices, -1), plane * PLANE, PLANE, axis=0)
+    rows = PLANE * vehicles_here
+    by_block = lambda x: lax.dynamic_slice_in_dim(x, plane * rows, rows, axis=0).reshape(PLANE, -1)
     sender = by_block(senders)
     shift = by_block(shifts)
     live = jnp.arange(agents)[None, None, :] < by_block(counts)[:, :, None]

time: 156 us -> 153 us (0.981)
  Pallas kernels: 148 us -> 146 us
    pallas_call x1, Pallas kernels: 119 us -> 117 us  [join_stage(): pl.pallas_call(join_kernel, in_specs=[scalars] * 5 + [vectors] * 4, out_s...]
    dynamic_slice x2 -> x5, local copies, waits for them, and re-layouts: 0.08 us -> 1.79 us  [route(): lax.dynamic_slice_in_dim(x, plane * rows, rows, axis=0).reshape(PLANE, -1)]
    unnamed x2, local copies, waits for them, and re-layouts: 1.68 us -> 0.01 us
where the time goes in v5:
time: 153 us
  Pallas kernels  146 us (95%)
  local copies, waits for them, and re-layouts  4.21 us (3%)
  other arithmetic  2.51 us (2%)
    pallas_call x1, Pallas kernels, join_stage(): pl.pallas_call(join_kernel, in_specs=[scalars] * 5 + [vectors] * 4, out_s...  117 us
    pallas_call x1, Pallas kernels, layer_stage(): pl.pallas_call(layer_kernel, grid=(vehicles,), in_specs=[block, block, ed...  29.3 us

profile of v5, /device:TPU:1, one launch (start us, length us, event | category | flops | bytes accessed | tf_op | source)
XLA Modules:
  0.0 152.8 jit_solution(5220422237308854396)
XLA Ops:
  0.0 0.8 dynamic_slice.24
  0.8 0.7 and_select_fusion.3
  1.5 0.1 constant_dynamic-slice_fusion.4
  1.5 0.8 constant_dynamic-slice_fusion.3
  2.4 0.1 lt.114
  2.5 0.1 lt.112
  2.7 0.1 copy.25
  2.8 0.1 reshape.425
  2.8 0.1 copy.22
  2.9 0.1 reshape.424
  3.1 0.3 select_reduce_fusion
  3.4 0.1 and.188
  3.6 0.1 squeeze.10
  3.7 0.1 squeeze.11
  3.8 0.1 add.210
  3.9 0.7 reshape.434.slot_ref
  4.6 0.6 reshape.437.bias_ref
  5.2 0.4 select_reduce_fusion.1
  5.6 0.4 multiply_reduce_fusion
  6.0 0.1 copy.26
  6.1 0.1 reshape.426
  6.2 0.6 and_select_fusion
  6.8 116.8 %join_stage.1 = (bf16[8,8,2,2,16,128]{5,4,3,2,1,0:T(8,128)(2,1)}, bf16[8,2,2,16,128]{4,3,2,1,0:T(8,128)(2,1)}, bf16[8,2,2,16,128]{4,3,2,1,0:T(8,128)(2,1)}, bf16...) custom-call(s32[128]{0:T(128)} %get-tuple-element.24.vehicle_ref, s32[128]{0:T(128)} %get-tuple-element.23.tile_ref, ...), custom_call_target="tpu_custom_call" | custom-call | tf_op jit(solution)/shard_map/join_stage/pallas_call | solution.py:382
  123.6 29.3 %layer_stage.1 = bf16[8,8,64,256]{3,2,1,0:T(8,128)(2,1)} custom-call(bf16[8,8,64,128]{3,2,1,0:T(8,128)(2,1)} %bev_ref.1, bf16[8,8,64,128]{3,2,1,0:T(8,128)(2,1)} %bitcast.10, bf16[8,1,64,128]{3,2,1,0:T(8,128)(2,1)} %bitcast.11, bf16[8,1,64,128]{3,2,1,0:T(8,128)(2,1)} %bitcast.12, bf16[8,1,64,128]{3,2,1,0:T(8,128)(2,1)} %bitcast.13, ...), custom_call_target="tpu_custom_call" | custom-call | tf_op jit(solution)/shard_map/layer_stage/pallas_call | solution.py:153
  (19 shorter events, 0.5 us)
Async XLA Ops:
  0.0 1.4 copy-start

commit v6 on v5

--- a/solution.py
+++ b/solution.py
@@ -123,7 +123,7 @@
             attended = jnp.where(lane_head == j, mixed_values[j * area : (j + 1) * area], attended)
         attended_ref[span, g * channels : (g + 1) * channels] = attended.astype(bf16)
 
-    units = [(w, g) for w in range(windows) for g in range(len(groups))]
+    units = [(w, g) for g in range(len(groups)) for w in range(windows)]
     all_scores = [score_of(w, g) for w, g in units]
     all_weights = [soften(s) for s in all_scores]
     for (w, g), weight in zip(units, all_weights):
@@ -271,7 +271,7 @@
     def attend(piece, vehicle):
         agents = bias_ref.shape[0] // (vehicles * tile_cols)
         member = member_matrix(channels)
-        row = lambda t, a: (vehicle * tile_cols + t) * agents + a
+        row = lambda t, a: (vehicle * agents + a) * tile_cols + t
         sent = [
             flat(inboxes[piece][slot_ref[row(t, a)]]) for a in range(agents) for t in range(tile_cols)
         ]
@@ -439,8 +439,7 @@
     slots = ((rank * PLANE + my_source % PLANE) * SLOTS + my_start)[:, None] + tile_step[None, :]
     slots = slots - jnp.maximum(-my_shift, 0)[:, None]
     slots = jnp.where(inside, slots, 0)
-    per_tile = lambda x: x.reshape(vehicles_here, agents, tile_cols).transpose(0, 2, 1).reshape(-1, agents)
-    return picks, per_tile(slots), per_tile(jnp.where(inside, 0.0, -1e30))
+    return picks, slots, jnp.where(inside, 0.0, -1e30)
 
 
 def on_device(bev_maps, senders, shifts, counts, agent_query, agent_keyvalue, agent_out, agent_scale,

time: 153 us -> 152 us (level)
  no operation moved by 1% of the time
where the time goes in v6:
time: 152 us
  Pallas kernels  146 us (96%)
  local copies, waits for them, and re-layouts  3.86 us (3%)
  other arithmetic  2.64 us (2%)
    pallas_call x1, Pallas kernels, join_stage(): pl.pallas_call(join_kernel, in_specs=[scalars] * 5 + [vectors] * 4, out_s...  117 us
    pallas_call x1, Pallas kernels, layer_stage(): pl.pallas_call(layer_kernel, grid=(vehicles,), in_specs=[block, block, ed...  28.9 us

profile of v6, /device:TPU:1, one launch (start us, length us, event | category | flops | bytes accessed | tf_op | source)
XLA Modules:
  0.0 152.3 jit_solution(11383716051710561614)
XLA Ops:
  0.0 0.8 dynamic_slice.24
  0.8 0.7 and_select_fusion.6
  1.5 0.1 constant_dynamic-slice_fusion.4
  1.5 0.8 constant_dynamic-slice_fusion.3
  2.4 0.1 lt.110
  2.4 0.1 copy.23
  2.5 0.1 lt.108
  2.7 0.1 copy.25
  2.8 0.1 reshape.386
  2.8 0.1 copy.22
  2.9 0.1 reshape.385
  3.1 0.3 select_reduce_fusion
  3.4 0.1 broadcast_compare_fusion
  3.5 0.4 select_reduce_fusion.1
  3.9 0.4 multiply_reduce_fusion
  4.2 0.1 subtract_select_fusion
  4.3 0.7 reshape.395.slot_ref
  5.0 0.1 broadcast_select_fusion
  5.1 0.6 reshape.398.bias_ref
  5.7 0.1 copy.26
  5.9 0.1 reshape.387
  6.0 0.6 and_select_fusion.3
  6.6 116.8 %join_stage.1 = (bf16[8,8,2,2,16,128]{5,4,3,2,1,0:T(8,128)(2,1)}, bf16[8,2,2,16,128]{4,3,2,1,0:T(8,128)(2,1)}, bf16[8,2,2,16,128]{4,3,2,1,0:T(8,128)(2,1)}, bf16...) custom-call(s32[128]{0:T(128)} %get-tuple-element.26.vehicle_ref, s32[128]{0:T(128)} %get-tuple-element.25.tile_ref, ...), custom_call_target="tpu_custom_call" | custom-call | tf_op jit(solution)/shard_map/join_stage/pallas_call | solution.py:382
  123.3 28.9 %layer_stage.1 = bf16[8,8,64,256]{3,2,1,0:T(8,128)(2,1)} custom-call(bf16[8,8,64,128]{3,2,1,0:T(8,128)(2,1)} %bev_ref.1, bf16[8,8,64,128]{3,2,1,0:T(8,128)(2,1)} %bitcast.23, bf16[8,1,64,128]{3,2,1,0:T(8,128)(2,1)} %bitcast.24, bf16[8,1,64,128]{3,2,1,0:T(8,128)(2,1)} %bitcast.25, bf16[8,1,64,128]{3,2,1,0:T(8,128)(2,1)} %bitcast.26, ...), custom_call_target="tpu_custom_call" | custom-call | tf_op jit(solution)/shard_map/layer_stage/pallas_call | solution.py:153
  (12 shorter events, 0.2 us)
Async XLA Ops:
  0.0 1.4 copy-start
